TPU v7x, 128 devices: a whole 4x4x4 slice. The times are simulated.
128 devices in a mesh: row: 16 (over x, z), col: 8 (over y, core).
Axes of the slice: x: 4, y: 4, z: 4, core: 2. Of those that a mesh axis runs over, the one named last changes fastest.
Arguments:
- gradient: bfloat16 [3072, 14336], P('row', 'col'), may hold values from -0.1875 to 0.1875
- left_factor: float32 [3072, 3072], P('row', 'col'), may hold values from -1 to 11, as said below
- right_factor: float32 [14336, 14336], P('col', 'row'), may hold values from -1 to 3, as said below
- left_basis: bfloat16 [3072, 3072], P('row', 'col'), may hold values from -0.109375 to 0.109375
- right_basis: bfloat16 [14336, 2048], P('row', 'col'), may hold values from -0.046875 to 0.046875
Outputs:
- left_new: float32 [3072, 3072], P('row', 'col')
- right_new: float32 [14336, 14336], P('col', 'row')
- left_out: float32 [3072, 3072], P('row', 'col')
- right_out: float32 [14336, 2048], P('col', 'row')
Inputs may be any that keep to these rules, and one draw needn't show every extreme that they name: left_factor is symmetric. right_factor is symmetric.
All inputs are finite; a program needn't handle non-finite values.
Results may differ from a plain program's by a relative error of at most 0.0029.
Values may be sent and summed in bfloat16 or wider, within the bound.
A program may use at most 128 MiB of HBM per device.

v0:
```python
import functools

import jax
import jax.numpy as jnp
from jax import lax
from jax.sharding import Mesh
from jax.sharding import PartitionSpec as P

DMODEL = 3072
DHIDDEN = 14336
ROW = ("row_0", "row_1")


ema_decay = 0.95
epsilon = 1e-06


def cut_along(value, dim, size):
    shape = value.shape
    parts = value.reshape(*shape[:dim], size, shape[dim] // size, *shape[dim + 1 :])
    return jnp.moveaxis(parts, dim, 0)


def summed_on_arrival(value, axis, dim):
    size = lax.axis_size(axis)
    parts = lax.all_to_all(cut_along(value, dim, size), axis, 0, 0, tiled=True)
    return jnp.sum(parts, axis=0)


def filled_up(lines, size):
    spare = -lines.shape[0] % size
    if not spare:
        return lines
    return jnp.concatenate([lines, jnp.zeros((spare, *lines.shape[1:]), lines.dtype)])


def from_root(value, axis, root):
    lines = jnp.where(lax.axis_index(axis) == root, value, jnp.zeros_like(value)).reshape(
        -1, *value.shape[1:][-1:]
    )
    padded = filled_up(lines, lax.axis_size(axis))
    own = lax.psum_scatter(padded, axis, scatter_dimension=0, tiled=True)
    return lax.all_gather(own, axis, axis=0, tiled=True)[: len(lines)].reshape(value.shape)


def in_order(parts, dim):
    parts = jnp.moveaxis(parts, 0, dim)
    shape = parts.shape
    return parts.reshape(*shape[:dim], shape[dim] * shape[dim + 1], *shape[dim + 2 :])


def sent_to_all(value, axis):
    size = lax.axis_size(axis)
    return lax.all_to_all(
        jnp.broadcast_to(value[None], (size, *value.shape)), axis, 0, 0, tiled=True
    )


def gather_directly(value, axis, dim):
    return in_order(sent_to_all(value, axis), dim)


def over_axes(value, axes):
    return functools.reduce(lax.psum, axes, value)


def taken_together(value, axis):
    return sent_to_all(value, axis).sum(axis=0)


def on_device(gradient, left_factor, right_factor, left_basis, right_basis):
    row_count = lax.axis_size(ROW)
    col_count = lax.axis_size("col")
    row_index = lax.axis_index(ROW)
    column_slab = lax.all_gather(gradient, ROW, axis=0, tiled=True)
    gram_block = summed_on_arrival(
        lax.dot_general(
            column_slab, gradient, (((1,), (1,)), ((), ())), preferred_element_type=jnp.float32
        ),
        "col",
        0,
    ).T
    left_new = ema_decay * left_factor + (1.0 - ema_decay) * gram_block
    group_ratio = row_count // col_count
    slab_cols = gradient.shape[1] // group_ratio
    offered = lax.dynamic_slice_in_dim(
        column_slab, row_index % group_ratio * slab_cols, slab_cols, 1
    )
    shared = from_root(offered, "col", row_index // group_ratio)
    right_block = lax.dot_general(
        column_slab, shared, (((0,), (0,)), ((), ())), preferred_element_type=jnp.float32
    )
    right_new = ema_decay * right_factor + (1.0 - ema_decay) * right_block
    left_half = left_new.astype(jnp.bfloat16)
    left_rows = gather_directly(left_half, "col", 1)
    left_prod = jnp.dot(
        left_rows, gather_directly(left_basis, ROW, 0), preferred_element_type=jnp.float32
    )
    right_half = right_new.astype(jnp.bfloat16)
    basis_full = lax.all_gather(right_basis, "col", axis=1, tiled=True)
    right_prod = lax.psum_scatter(
        lax.dot_general(
            basis_full, right_half, (((0,), (1,)), ((), ())), preferred_element_type=jnp.float32
        ),
        ROW,
        scatter_dimension=0,
        tiled=True,
    ).T
    left_sq = jnp.sum(left_prod * left_prod, axis=0)
    right_sq = jnp.sum(right_prod * right_prod, axis=0)
    left_sq = over_axes(left_sq, ROW)
    right_sq = taken_together(right_sq, "col")
    left_out = left_prod * lax.rsqrt(left_sq / DMODEL + epsilon)
    right_out = right_prod * lax.rsqrt(right_sq / DHIDDEN + epsilon)
    return (left_new, right_new, left_out, right_out)


def solution(mesh):
    split = Mesh(mesh.devices.reshape(4, 4, mesh.shape["col"]), ("row_0", "row_1", "col"))
    in_specs = (P(ROW, "col"), P(ROW, "col"), P("col", ROW), P(ROW, "col"), P(ROW, "col"))
    out_specs = (P(ROW, "col"), P("col", ROW), P(ROW, "col"), P("col", ROW))
    return jax.shard_map(
        on_device, mesh=split, in_specs=in_specs, out_specs=out_specs, check_vma=False
    )
```

profile of v0, /device:TPU:1, one launch (start us, length us, event | category | flops | bytes accessed | tf_op | source)
XLA Modules:
  0.0 386.5 jit_solution(1360049100948953040)
XLA Ops:
  7.2 0.0 all-gather.4.cloned.1.call-start
  7.2 0.7 all-gather.4.cloned.1.call-update
  7.9 0.0 reduce-scatter.3.cloned.1.call-start
  8.0 88.0 %all-gather.4.cloned.1.call-done = bf16[3072,1792]{1,0:T(8,128)(2,1)} async-done(((bf16[192,1792]{1,0:T(8,128)(2,1)}), bf16[3072,1792]{1,0:T(8,128)(2,1)}) %all-gather.4.cloned.1.call-update) | async-done | bytes 11010064 | tf_op jit(solution)/shard_map/all_gather | solution.py:75
  96.0 6.0 %dynamic-slice_select_fusion = bf16[3072,896]{1,0:T(8,128)(2,1)} fusion(bf16[3072,1792]{1,0:T(8,128)(2,1)} %all-gather.4.cloned.1.call-done, s32[]{:T(128)S(6)} %select_n.25, pred[]{:T(512)S(6)} %eq.5), kind=kLoop, calls=%fused_computation.2 | loop fusion | flops 2752512 | bytes 11010053 | tf_op jit(solution)/shard_map/jit(_where)/select_n | solution.py:38
  102.0 0.0 reduce-scatter.3.cloned.1.call-update
  102.0 0.0 all-gather.6.cloned.1.call-start
  102.1 38.0 %reduce-scatter.3.cloned.1.call-done = bf16[384,896]{1,0:T(8,128)(2,1)} async-done(((bf16[3072,896]{1,0:T(8,128)(2,1)}), bf16[384,896]{1,0:T(8,128)(2,1)}) %reduce-scatter.3.cloned.1.call-update) | async-done | bytes 688144 | tf_op jit(solution)/shard_map/reduce_scatter | solution.py:42
  140.1 0.0 all-gather.6.cloned.1.call-update
  140.1 0.0 all-gather.8.cloned.1.call-start
  140.2 0.5 all-gather.8.cloned.1.call-update
  140.7 0.0 reduce-scatter.5.cloned.1.call-start
  140.8 7.8 %copy.22 = f32[1792,896]{0,1:T(8,128)} copy(f32[1792,896]{1,0:T(8,128)} %param.7) | data formatting | bytes 12845056 | tf_op args[2]
  148.5 33.1 %all-gather.6.cloned.1.call-done = bf16[3072,896]{1,0:T(8,128)(2,1)} async-done(((bf16[384,896]{1,0:T(8,128)(2,1)}), bf16[3072,896]{1,0:T(8,128)(2,1)}) %all-gather.6.cloned.1.call-update) | async-done | bytes 5505040 | tf_op jit(solution)/shard_map/all_gather | solution.py:43
  181.7 18.8 %bitcast_add_fusion = f32[1792,896]{0,1:T(8,128)} fusion(f32[1792,896]{0,1:T(8,128)} %copy.22, bf16[3072,896]{1,0:T(8,128)(2,1)} %all-gather.6.cloned.1.call-done, bf16[3072,1792]{1,0:T(8,128)(2,1)} %all-gather.4.cloned.1.call-done), kind=kOutput, calls=%fused_computation.1 | convolution fusion | flops 9869819904 | bytes 29360128 | tf_op jit(solution)/shard_map/dot_general | solution.py:90
  200.5 16.1 %all-gather.8.cloned.1.call-done = bf16[896,2048]{1,0:T(8,128)(2,1)} async-done(((bf16[896,256]{1,0:T(8,128)(2,1)}), bf16[896,2048]{1,0:T(8,128)(2,1)}) %all-gather.8.cloned.1.call-update) | async-done | bytes 3670032 | tf_op jit(solution)/shard_map/all_gather | solution.py:100
  216.6 14.3 %convolution_bitcast_fusion = f32[2048,1792]{0,1:T(8,128)} fusion(bf16[896,2048]{1,0:T(8,128)(2,1)} %all-gather.8.cloned.1.call-done, f32[1792,896]{0,1:T(8,128)} %bitcast_add_fusion), kind=kOutput, calls=%fused_computation | convolution fusion | flops 6578274304 | bytes 24772608 | tf_op jit(solution)/shard_map/dot_general | solution.py:102
  230.9 0.0 copy-start.1
  230.9 0.0 reduce-scatter.5.cloned.1.call-update
  230.9 1.1 copy-done.1
  232.0 7.8 %fusion.2 = f32[3072,192]{0,1:T(8,128)S(1)} fusion(bf16[3072,1792]{1,0:T(8,128)(2,1)} %all-gather.4.cloned.1.call-done, bf16[192,1792]{1,0:T(8,128)(2,1)S(1)} %copy-done.1), kind=kOutput, calls=%fused_computation.13 | convolution fusion | flops 2113929216 | bytes 14057472 | tf_op jit(solution)/shard_map/dot_general | solution.py:77
  239.8 0.0 copy-start.2
  239.8 0.2 copy.29
  240.0 0.0 copy-start.3
  240.0 33.1 %all_to_all.21 = f32[8,384,192]{1,2,0:T(8,128)S(1)} all-to-all(f32[8,384,192]{1,2,0:T(8,128)S(1)} %bitcast.25), channel_id=1, replica_groups=mesh['row_0'=4,'row_1'=4,'col'=8] {'col'}, dimensions={0} | all-to-all | bytes 4718592 | tf_op jit(solution)/shard_map/all_to_all | solution.py:26
  273.1 0.1 reduce_sum.36
  273.3 0.0 copy-done.2
  273.3 0.8 fusion.1
  274.0 0.1 broadcast_in_dim.9
  274.1 20.0 %all_to_all.22 = bf16[8,192,384]{2,1,0:T(8,128)(2,1)S(1)} all-to-all(bf16[8,192,384]{2,1,0:T(8,128)(2,1)S(1)} %broadcast_in_dim.9), channel_id=1, replica_groups=mesh['row_0'=4,'row_1'=4,'col'=8] {'col'}, dimensions={0} | all-to-all | bytes 2359296 | tf_op jit(solution)/shard_map/all_to_all | solution.py:54
  294.2 0.0 copy-done.3
  294.2 1.7 broadcast_in_dim.10
  295.9 6.6 %all-to-all-start.2 = ((bf16[16,192,384]{2,1,0:T(8,128)(2,1)}), bf16[16,192,384]{2,1,0:T(8,128)(2,1)S(1)}, u32[]{:S(2)}, u32[]{:S(2)}) async-start(bf16[16,192,384]{2,1,0:T(8,128)(2,1)} %broadcast_in_dim.10), calls=%async_computation.3 | async-start | bytes 4718592 | tf_op jit(solution)/shard_map/all_to_all | solution.py:54
  302.5 1.2 copy.27
  303.7 34.3 %all-to-all-done.2 = bf16[16,192,384]{2,1,0:T(8,128)(2,1)S(1)} async-done(((bf16[16,192,384]{2,1,0:T(8,128)(2,1)}), bf16[16,192,384]{2,1,0:T(8,128)(2,1)S(1)}, u32[]{:S(2)}, u32[]{:S(2)}) %all-to-all-start.2) | async-done | bytes 2359328 | tf_op jit(solution)/shard_map/all_to_all | solution.py:54
  338.1 2.1 multiply_reduce_fusion.1
  340.1 6.7 %psum.14 = f32[384]{0:T(512)S(1)} all-reduce(f32[384]{0:T(512)S(1)} %get-tuple-element.26), channel_id=1, replica_groups=mesh['row_0'=4,'row_1'=4,'col'=8] {'row_0'}, use_global_device_ids=true, to_apply=%region_3.4 | all-reduce | flops 384 | bytes 3072 | tf_op jit(solution)/shard_map/psum | solution.py:64
  346.8 10.1 %psum.15 = f32[384]{0:T(512)S(1)} all-reduce(f32[384]{0:T(512)S(1)} %psum.14), channel_id=1, replica_groups=mesh['row_0'=4,'row_1'=4,'col'=8] {'row_1'}, use_global_device_ids=true, to_apply=%region_4.5 | all-reduce | flops 384 | bytes 3072 | tf_op jit(solution)/shard_map/psum | solution.py:64
  356.8 0.0 reduce-scatter.5.cloned.1.call-done
  356.8 1.4 multiply_reduce_fusion
  358.3 0.6 broadcast_in_dim.11
  358.9 11.5 %all-to-all-start.3 = ((f32[8,1,128]{2,1,0:T(1,128)}), f32[8,1,128]{2,1,0:T(1,128)S(1)}, u32[]{:S(2)}, u32[]{:S(2)}) async-start(f32[8,1,128]{2,1,0:T(1,128)} %broadcast_in_dim.11), calls=%async_computation.5 | async-start | bytes 8192 | tf_op jit(solution)/shard_map/all_to_all | solution.py:54
  370.4 0.7 broadcast_multiply_fusion
  371.1 0.0 copy-start
  371.1 7.9 %copy.25 = f32[1792,896]{1,0:T(8,128)} copy(f32[1792,896]{0,1:T(8,128)} %bitcast_add_fusion) | data formatting | bytes 12845056
  379.0 0.0 all-to-all-done.3
  379.0 0.0 copy-done
  379.0 1.0 multiply_bitcast_fusion
  (3 shorter events, 0.0 us)
Async XLA Ops:
  7.2 88.8 %all-gather.4.cloned.1.call-start = ((), (), s32[]{:S(2)}) async-start(), calls=%async_computation.6 | async-start | bytes 11698176 | tf_op jit(solution)/shard_map/all_gather | solution.py:75
  7.9 132.2 %reduce-scatter.3.cloned.1.call-start = ((), (), s32[]{:S(2)}) async-start(), calls=%async_computation.7 | async-start | bytes 6193152 | tf_op jit(solution)/shard_map/reduce_scatter | solution.py:42
  102.0 79.7 %all-gather.6.cloned.1.call-start = ((), (), s32[]{:S(2)}) async-start(), calls=%async_computation.8 | async-start | bytes 6193152 | tf_op jit(solution)/shard_map/all_gather | solution.py:43
  140.1 76.4 %all-gather.8.cloned.1.call-start = ((), (), s32[]{:S(2)}) async-start(), calls=%async_computation.9 | async-start | bytes 4128768 | tf_op jit(solution)/shard_map/all_gather | solution.py:100
  140.7 216.1 %reduce-scatter.5.cloned.1.call-start = ((), (), s32[]{:S(2)}) async-start(), calls=%async_computation.10 | async-start | bytes 15597568 | tf_op jit(solution)/shard_map/reduce_scatter | solution.py:101
  230.9 1.1 copy-start.1
  239.8 33.4 %copy-start.2 = (f32[192,384]{1,0:T(8,128)S(1)}, f32[192,384]{1,0:T(8,128)}, u32[]{:S(2)}) copy-start(f32[192,384]{1,0:T(8,128)} %param.6) | copy-start | bytes 884740
  240.0 54.2 %copy-start.3 = (bf16[192,384]{1,0:T(8,128)(2,1)S(1)}, bf16[192,384]{1,0:T(8,128)(2,1)}, u32[]{:S(2)}) copy-start(bf16[192,384]{1,0:T(8,128)(2,1)} %param.8) | copy-start | bytes 442372
  295.9 42.2 %all-to-all-start.2 = ((bf16[16,192,384]{2,1,0:T(8,128)(2,1)}), bf16[16,192,384]{2,1,0:T(8,128)(2,1)S(1)}, u32[]{:S(2)}, u32[]{:S(2)}) async-start(bf16[16,192,384]{2,1,0:T(8,128)(2,1)} %broadcast_in_dim.10), calls=%async_computation.3 | async-start | bytes 4718592 | tf_op jit(solution)/shard_map/all_to_all | solution.py:54
  358.9 20.1 %all-to-all-start.3 = ((f32[8,1,128]{2,1,0:T(1,128)}), f32[8,1,128]{2,1,0:T(1,128)S(1)}, u32[]{:S(2)}, u32[]{:S(2)}) async-start(f32[8,1,128]{2,1,0:T(1,128)} %broadcast_in_dim.11), calls=%async_computation.5 | async-start | bytes 8192 | tf_op jit(solution)/shard_map/all_to_all | solution.py:54
  371.1 7.9 %copy-start = (f32[128,1792]{0,1:T(8,128)S(1)}, f32[128,1792]{0,1:T(8,128)}, u32[]{:S(2)}) copy-start(f32[128,1792]{0,1:T(8,128)} %reduce-scatter.5.cloned.1.call-done) | copy-start | bytes 2752516
Sparse Core Ops, SparseCore 0:
  10.2 85.8 all-gather.3
  102.1 37.9 reduce-scatter.2
  141.8 39.8 all-gather.5
  183.2 33.3 all-gather.7
  231.1 119.6 reduce-scatter.4
where the time goes:
time: 387 us
  waiting for transfers between devices  211 us (55%)
  blocking collectives  69.8 us (18%)
  matrix products  43 us (11%)
  local copies, waits for them, and re-layouts  20.5 us (5%)
  starting transfers between devices  18.3 us (5%)
  between operations  13.9 us (4%)
  other arithmetic  10.1 us (3%)
    all_gather x1, waiting for transfers between devices, on_device(): column_slab = lax.all_gather(gradient, ROW, axis=0, tiled=True)  88 us
    reduce_scatter x1, waiting for transfers between devices, from_root(): own = lax.psum_scatter(padded, axis, scatter_dimension=0, tiled=True)  38 us
    all_to_all x2, waiting for transfers between devices, sent_to_all(): lax.all_to_all(jnp.broadcast_to(value[None], (size, *value.shape)), axis,...  34.3 us
    all_gather x1, waiting for transfers between devices, from_root(): lax.all_gather(own, axis, axis=0, tiled=True)[:len(lines)]  33.1 us
    all_to_all x1, blocking collectives, summed_on_arrival(): parts = lax.all_to_all(cut_along(value, dim, size), axis, 0, 0, tiled=True)  33.1 us
    all_to_all x1, blocking collectives, sent_to_all(): lax.all_to_all(jnp.broadcast_to(value[None], (size, *value.shape)), axis,...  20 us
    dot_general x1, matrix products, on_device(): lax.dot_general(column_slab, shared, (((0,), (0,)), ((), ())), preferred_...  18.8 us
    all_to_all x2, starting transfers between devices, sent_to_all(): lax.all_to_all(jnp.broadcast_to(value[None], (size, *value.shape)), axis,...  18.1 us
  transfers between devices with their start and end apart: 7, of which 5 were waited for; matrix products, arithmetic and copies ran while one was open for 13% of the time, Pallas kernels for 0%

commit v1 on v0

v1 whole, which is shorter than its diff:
```python
import functools

import jax
import jax.numpy as jnp
from jax import lax
from jax.experimental import pallas as pl
from jax.experimental.pallas import tpu as pltpu
from jax.sharding import PartitionSpec as P

DMODEL = 3072
DHIDDEN = 14336
ema_decay = 0.95
epsilon = 1e-06
MESH = pl.DeviceIdType.MESH
F32 = jnp.float32
BF16 = jnp.bfloat16
GC = 1792
LC = 384
W = GC + LC
SC = 896
FIRST, SECOND = "f", "s"


def wrap(v):
    return (v + 1) % 4 - 1


def message_table():
    keys = []
    for h in (0, 1):
        for axis in (FIRST, SECOND):
            for d in (1, -1):
                keys.append((h, 0, 0, "full", axis, d))
        keys.append((h, -1, 0, 0, FIRST, 1))
        keys.append((h, 1, 0, 1, FIRST, -1))
        for df in (-1, 1, 2):
            for d in (1, -1):
                keys.append((h, df, 0, "full", SECOND, d))
        for df in (0, -1, 1, 2):
            keys.append((h, df, -1, 0, SECOND, 1))
            keys.append((h, df, 1, 1, SECOND, -1))
    return {key: i for i, key in enumerate(keys)}


AG = message_table()
UNITS = [
    [(0, 0)],
    [(-1, 0), (1, 0)],
    [(0, -1), (0, 1)],
    [(2, 0)],
    [(-1, -1), (1, -1), (-1, 1), (1, 1)],
    [(0, 2)],
    [(2, -1), (2, 1)],
    [(-1, 2), (1, 2)],
    [(2, 2)],
]


def gather_kernel(
    grad, lbas, rbas, acc_o, bas_o, lb_o, lp_o,
    slab, shared, acc, bas, lp,
    ag_s, ag_r, y_s, y_r, sib_s, sib_r, loc, bs, br, bss, bsr, cp,
):
    row = lax.axis_index("row")
    col = lax.axis_index("col")
    x, z = row // 4, row % 4
    y, k = col // 2, col % 2
    sib = {"col": y * 2 + (1 - k)}

    def ydev(d):
        return {"col": ((y + d + 4) % 4) * 2 + k}

    def rid(dx, dz):
        return ((x + dx + 4) % 4) * 4 + (z + dz + 4) % 4

    def region(ref, h, df, ds, part):
        dx, dz = (df, ds) if h == 0 else (ds, df)
        q, n = (0, 2) if part == "full" else (part, 1)
        return ref.at[pl.ds(rid(dx, dz) * 4 + 2 * h + q, n)]

    def neighbour(h, axis, d):
        if (h == 0) == (axis == FIRST):
            return {"row": ((x + d + 4) % 4) * 4 + z}
        return {"row": x * 4 + (z + d + 4) % 4}

    def ag(h, df, ds, part, axis, d):
        i = AG[(h, df, ds, part, axis, d)]
        ref = region(slab, h, df, ds, part)
        return pltpu.make_async_remote_copy(
            src_ref=ref, dst_ref=ref, send_sem=ag_s.at[i], recv_sem=ag_r.at[i],
            device_id=neighbour(h, axis, d), device_id_type=MESH,
        )

    def ag_wait(h, df, ds, part, axis, d):
        key = (h, wrap(df + d), ds, part, axis, d) if axis == FIRST else (h, df, wrap(ds + d), part, axis, d)
        i = AG[key]
        ref = region(slab, h, df, ds, part)
        pltpu.make_async_remote_copy(
            src_ref=ref, dst_ref=ref, send_sem=ag_s.at[i], recv_sem=ag_r.at[i],
            device_id=neighbour(h, axis, d), device_id_type=MESH,
        ).wait_recv()

    own = [
        pltpu.make_async_copy(grad, slab.at[pl.ds(row * 4, 4), :, pl.ds(0, GC)], cp.at[0]),
        pltpu.make_async_copy(lbas, slab.at[pl.ds(row * 4, 4), :, pl.ds(GC, LC)], cp.at[1]),
        pltpu.make_async_copy(rbas, bas.at[col], cp.at[2]),
    ]
    for c in own:
        c.start()

    barrier = pltpu.get_barrier_semaphore()
    peers = [neighbour(0, a, d) for a in (FIRST, SECOND) for d in (1, -1)] + [ydev(1), ydev(-1), sib]
    for peer in peers:
        pl.semaphore_signal(barrier, inc=1, device_id=peer, device_id_type=MESH)
    for c in own:
        c.wait()
    pl.semaphore_wait(barrier, len(peers))

    is_k = k == z // 2
    role = (y - x + 4) % 4
    source = jnp.logical_and(is_k, role == 0)
    relay = jnp.logical_and(is_k, role != 0)
    c0 = pl.multiple_of((z % 2) * SC, 128)

    def unit_id(h, df, ds):
        return h * 16 + (df + 1) * 4 + ds + 1

    def unit_region(h, df, ds):
        return region(shared, h, df, ds, "full")

    def unit_src(h, df, ds):
        dx, dz = (df, ds) if h == 0 else (ds, df)
        return slab.at[pl.ds(rid(dx, dz) * 4 + 2 * h, 2), :, pl.ds(c0, SC)]

    def to_y(src, h, df, ds):
        i = unit_id(h, df, ds)
        return pltpu.make_async_remote_copy(
            src_ref=src, dst_ref=unit_region(h, df, ds), send_sem=y_s.at[i], recv_sem=y_r.at[i],
            device_id=ydev(1 if h == 0 else -1), device_id_type=MESH,
        )

    def to_sib(src, h, df, ds):
        i = unit_id(h, df, ds)
        return pltpu.make_async_remote_copy(
            src_ref=src, dst_ref=unit_region(h, df, ds), send_sem=sib_s.at[i], recv_sem=sib_r.at[i],
            device_id=sib, device_id_type=MESH,
        )

    def local(h, df, ds):
        return pltpu.make_async_copy(unit_src(h, df, ds), unit_region(h, df, ds), loc.at[unit_id(h, df, ds)])

    def last_role(h):
        return 3 if h == 0 else 1

    def source_units(step):
        @pl.when(source)
        def _():
            for df, ds in UNITS[step]:
                for h in (0, 1):
                    src = unit_src(h, df, ds)
                    to_y(src, h, df, ds).start()
                    to_sib(src, h, df, ds).start()
                    local(h, df, ds).start()

    def relay_units(step):
        @pl.when(relay)
        def _():
            for df, ds in UNITS[step]:
                for h in (0, 1):
                    ref = unit_region(h, df, ds)
                    to_y(ref, h, df, ds).wait_recv()

                    @pl.when(role != last_role(h))
                    def _():
                        to_y(ref, h, df, ds).start()

                    to_sib(ref, h, df, ds).start()

    def b_ref(dy, kk, part):
        c = ((y + dy + 4) % 4) * 2 + kk
        return bas.at[c] if part == "full" else bas.at[c, part]

    def b_send(i, dy, part, d):
        ref = b_ref(dy, k, part)
        return pltpu.make_async_remote_copy(
            src_ref=ref, dst_ref=ref, send_sem=bs.at[i], recv_sem=br.at[i], device_id=ydev(d), device_id_type=MESH,
        )

    def b_sib(i, dy, kk):
        ref = b_ref(dy, kk, "full")
        return pltpu.make_async_remote_copy(
            src_ref=ref, dst_ref=ref, send_sem=bss.at[i], recv_sem=bsr.at[i], device_id=sib, device_id_type=MESH,
        )

    def group(dx, first, last):
        xg = (x + dx + 4) % 4
        units = [(0, dx, dz) for dz in (-1, 0, 1, 2)] + [(1, dz, dx) for dz in (-1, 0, 1, 2)]

        @pl.when(jnp.logical_not(is_k))
        def _():
            for u in units:
                to_sib(unit_region(*u), *u).wait_recv()

        @pl.when(source)
        def _():
            for u in units:
                local(*u).wait()

        rows = pl.ds(xg * 16, 16)

        def tile(m, carry):
            cols = pl.ds(pl.multiple_of(m * 256, 256), 256)
            a = slab[rows, :, cols].reshape(768, 256)
            b = shared[rows].reshape(768, SC)
            d = lax.dot_general(a, b, (((0,), (0,)), ((), ())), preferred_element_type=F32)
            if first:
                acc[m] = d
            else:
                acc[m] = acc[m] + d
            if last:
                pltpu.make_async_copy(acc.at[m], acc_o.at[m], cp.at[m]).start()
            return carry

        lax.fori_loop(0, 7, tile, 0)

        def left(j, carry):
            a = slab[pl.ds(row * 4, 4), :, pl.ds(0, GC)].reshape(192, GC)
            b = slab[pl.ds(xg * 16 + j * 8, 8), :, pl.ds(0, GC)].reshape(384, GC)
            d = lax.dot_general(a, b, (((1,), (1,)), ((), ())), preferred_element_type=F32)
            lp[xg * 2 + j] = d.astype(BF16)
            return carry

        lax.fori_loop(0, 2, left, 0)

    sent = []

    def go(*key):
        c = ag(*key)
        c.start()
        sent.append(c)

    H = (0, 1)
    for axis in (FIRST, SECOND):
        for h in H:
            for d in (1, -1):
                go(h, 0, 0, "full", axis, d)
    b_sends = [b_send(0, 0, "full", 1), b_send(1, 0, "full", -1)]
    b_sibs = [b_sib(0, 0, k)]
    for c in b_sends + b_sibs:
        c.start()
    source_units(0)
    for h in H:
        ag_wait(h, -1, 0, "full", FIRST, 1)
        ag_wait(h, 1, 0, "full", FIRST, -1)
    for h in H:
        go(h, -1, 0, 0, FIRST, 1)
        go(h, 1, 0, 1, FIRST, -1)
    for df in (-1, 1):
        for h in H:
            for d in (1, -1):
                go(h, df, 0, "full", SECOND, d)
    source_units(1)
    relay_units(0)
    for h in H:
        ag_wait(h, 0, -1, "full", SECOND, 1)
        ag_wait(h, 0, 1, "full", SECOND, -1)
    for h in H:
        go(h, 0, -1, 0, SECOND, 1)
        go(h, 0, 1, 1, SECOND, -1)
    source_units(2)
    relay_units(1)
    b_send(0, -1, "full", 1).wait_recv()
    b_send(1, 1, "full", -1).wait_recv()
    more = [b_send(2, -1, 0, 1), b_send(3, 1, 1, -1)]
    more_sib = [b_sib(1, -1, k), b_sib(2, 1, k)]
    for c in more + more_sib:
        c.start()
    b_sends += more
    b_sibs += more_sib
    for h in H:
        ag_wait(h, 2, 0, 0, FIRST, 1)
        ag_wait(h, 2, 0, 1, FIRST, -1)
    for h in H:
        for d in (1, -1):
            go(h, 2, 0, "full", SECOND, d)
    source_units(3)
    relay_units(2)
    for df in (-1, 1):
        for h in H:
            ag_wait(h, df, -1, "full", SECOND, 1)
            ag_wait(h, df, 1, "full", SECOND, -1)
    for df in (-1, 1):
        for h in H:
            go(h, df, -1, 0, SECOND, 1)
            go(h, df, 1, 1, SECOND, -1)
    source_units(4)
    relay_units(3)
    b_send(2, 2, 0, 1).wait_recv()
    b_send(3, 2, 1, -1).wait_recv()
    c = b_sib(3, 2, k)
    c.start()
    b_sibs.append(c)
    for h in H:
        ag_wait(h, 0, 2, 0, SECOND, 1)
        ag_wait(h, 0, 2, 1, SECOND, -1)
    source_units(5)
    relay_units(4)
    for h in H:
        ag_wait(h, 2, -1, "full", SECOND, 1)
        ag_wait(h, 2, 1, "full", SECOND, -1)
    for h in H:
        go(h, 2, -1, 0, SECOND, 1)
        go(h, 2, 1, 1, SECOND, -1)
    source_units(6)
    relay_units(5)
    group(0, True, False)
    for df in (-1, 1):
        for h in H:
            ag_wait(h, df, 2, 0, SECOND, 1)
            ag_wait(h, df, 2, 1, SECOND, -1)
    source_units(7)
    relay_units(6)
    for h in H:
        ag_wait(h, 2, 2, 0, SECOND, 1)
        ag_wait(h, 2, 2, 1, SECOND, -1)
    source_units(8)
    lb_copy = pltpu.make_async_copy(slab.at[:, :, pl.ds(GC, LC)], lb_o, cp.at[7])
    lb_copy.start()
    relay_units(7)
    group(-1, False, False)
    relay_units(8)
    for i, dy in enumerate((0, -1, 1, 2)):
        b_sib(i, dy, 1 - k).wait_recv()
    bas_copy = pltpu.make_async_copy(bas, bas_o, cp.at[8])
    bas_copy.start()
    group(1, False, False)
    group(2, False, True)
    lp_copy = pltpu.make_async_copy(lp, lp_o, cp.at[9])
    lp_copy.start()

    for c in sent + b_sends + b_sibs:
        c.wait_send()
    for step in range(9):
        for df, ds in UNITS[step]:
            for h in H:
                ref = unit_region(h, df, ds)

                @pl.when(jnp.logical_and(is_k, jnp.logical_or(role == 0, role != last_role(h))))
                def _():
                    to_y(ref, h, df, ds).wait_send()

                @pl.when(is_k)
                def _():
                    to_sib(ref, h, df, ds).wait_send()

    for m in range(7):
        pltpu.make_async_copy(acc.at[m], acc_o.at[m], cp.at[m]).wait()
    lb_copy.wait()
    bas_copy.wait()
    lp_copy.wait()


def gather_all(gradient, left_basis, right_basis):
    dma = pltpu.SemaphoreType.DMA
    n = len(AG)
    any_spec = pl.BlockSpec(memory_space=pl.ANY)
    return pl.pallas_call(
        gather_kernel,
        out_shape=(
            jax.ShapeDtypeStruct((7, 256, SC), F32),
            jax.ShapeDtypeStruct((8, 2, 448, 256), BF16),
            jax.ShapeDtypeStruct((64, 48, LC), BF16),
            jax.ShapeDtypeStruct((8, 192, LC), BF16),
        ),
        in_specs=[any_spec] * 3,
        out_specs=[any_spec] * 4,
        scratch_shapes=[
            pltpu.VMEM((64, 48, W), BF16),
            pltpu.VMEM((64, 48, SC), BF16),
            pltpu.VMEM((7, 256, SC), F32),
            pltpu.VMEM((8, 2, 448, 256), BF16),
            pltpu.VMEM((8, 192, LC), BF16),
            dma((n,)), dma((n,)), dma((32,)), dma((32,)), dma((32,)), dma((32,)), dma((32,)),
            dma((4,)), dma((4,)), dma((4,)), dma((4,)), dma((10,)),
        ],
        compiler_params=pltpu.CompilerParams(
            collective_id=0, has_side_effects=True, vmem_limit_bytes=48 * 1024 * 1024
        ),
        name="gather_gram",
    )(gradient.reshape(4, 48, GC), left_basis.reshape(4, 48, LC), right_basis.reshape(2, 448, 256))


def product_kernel(acc, factor, basis, new, part):
    value = ema_decay * factor[...] + (1.0 - ema_decay) * acc[0]
    new[...] = value
    half = value.astype(BF16)
    for c in range(8):
        d = jnp.dot(half, basis[c], preferred_element_type=F32).astype(BF16)
        part[2 * c] = d[:, :128]
        part[2 * c + 1] = d[:, 128:]


def product(acc, factor, basis):
    return pl.pallas_call(
        product_kernel,
        grid=(7,),
        out_shape=(
            jax.ShapeDtypeStruct((GC, SC), F32),
            jax.ShapeDtypeStruct((16, GC, 128), BF16),
        ),
        in_specs=[
            pl.BlockSpec((1, 256, SC), lambda i: (i, 0, 0)),
            pl.BlockSpec((256, SC), lambda i: (i, 0)),
            pl.BlockSpec((8, SC, 256), lambda i: (0, 0, 0)),
        ],
        out_specs=(
            pl.BlockSpec((256, SC), lambda i: (i, 0)),
            pl.BlockSpec((16, 256, 128), lambda i: (0, i, 0)),
        ),
        compiler_params=pltpu.CompilerParams(vmem_limit_bytes=40 * 1024 * 1024),
        name="product",
    )(acc, factor, basis)


def on_device(gradient, left_factor, right_factor, left_basis, right_basis):
    acc, basis, lb, lp = gather_all(gradient, left_basis, right_basis)
    right_new, parts = product(acc, right_factor, basis.reshape(8, SC, 256))
    gram_block = jnp.sum(lax.all_to_all(lp, "col", 0, 0, tiled=True).astype(F32), axis=0)
    left_new = ema_decay * left_factor + (1.0 - ema_decay) * gram_block
    left_half = left_new.astype(BF16)
    left_rows = lax.all_gather(left_half, "col", axis=1, tiled=True)
    left_prod = jnp.dot(left_rows, lb.reshape(DMODEL, LC), preferred_element_type=F32)
    right_prod = jnp.sum(lax.all_to_all(parts, "row", 0, 0, tiled=True).astype(F32), axis=0)
    left_sq = lax.psum(jnp.sum(left_prod * left_prod, axis=0), "row")
    right_sq = lax.psum(jnp.sum(right_prod * right_prod, axis=0), "col")
    left_out = left_prod * lax.rsqrt(left_sq / DMODEL + epsilon)
    right_out = right_prod * lax.rsqrt(right_sq / DHIDDEN + epsilon)
    return (left_new, right_new, left_out, right_out)


def solution(mesh):
    in_specs = (P("row", "col"), P("row", "col"), P("col", "row"), P("row", "col"), P("row", "col"))
    out_specs = (P("row", "col"), P("col", "row"), P("row", "col"), P("col", "row"))
    return jax.shard_map(on_device, mesh=mesh, in_specs=in_specs, out_specs=out_specs, check_vma=False)
```

time: 387 us -> 573 us (1.48)
  Pallas kernels: 0 us -> 230 us
  waiting for transfers between devices: 211 us -> 26.7 us
  starting transfers between devices: 18.3 us -> 140 us
  blocking collectives: 69.8 us -> 143 us
  matrix products: 43 us -> 2.06 us
  local copies, waits for them, and re-layouts: 20.5 us -> 7.88 us
    pallas_call x0 -> x2, Pallas kernels: none -> 230 us  [the longest x1 218 us: gather_all(): pl.pallas_call(gather_kernel, out_shape=(jax.ShapeDtypeStruct((7, 256, SC...]
    psum x2, blocking collectives: 16.7 us -> 143 us  [the longest x1 123 us: on_device(): left_sq = lax.psum(jnp.sum(left_prod * left_prod, axis=0), 'row')]
    all_to_all x2, starting transfers between devices: 18.1 us -> 140 us  [the longest x1 115 us: on_device(): lax.all_to_all(lp, 'col', 0, 0, tiled=True).astype(F32)]
    all_gather x3 -> x1, waiting for transfers between devices: 137 us -> 26.7 us  [on_device(): left_rows = lax.all_gather(left_half, 'col', axis=1, tiled=True)]
    all_to_all x2 -> x0, blocking collectives: 53.1 us -> none  [the longest x1 33.1 us: summed_on_arrival(): parts = lax.all_to_all(cut_along(value, dim, size), axis, 0, 0, tiled=True)]
    dot_general x4 -> x1, matrix products: 43 us -> 2.06 us  [on_device(): jnp.dot(left_rows, lb.reshape(DMODEL, LC), preferred_element_type=F32)]
    reduce_scatter x2 -> x0, waiting for transfers between devices: 38 us -> none  [the longest x1 38 us: from_root(): own = lax.psum_scatter(padded, axis, scatter_dimension=0, tiled=True)]
    all_to_all x2, waiting for transfers between devices: 34.3 us -> 0.01 us  [the longest x1 0.01 us: on_device(): lax.all_to_all(parts, 'row', 0, 0, tiled=True).astype(F32)]
  transfers between devices with their start and end apart: 7 -> 3, of which waited for: 5 -> 1; matrix products, arithmetic and copies ran while one was open for 13% -> 1% of each run, Pallas kernels for 0% -> 2%
where the time goes in v1:
time: 573 us; the launch traced here: 572 us
  Pallas kernels  230 us (40%)
  blocking collectives  143 us (25%)
  starting transfers between devices  140 us (24%)
  waiting for transfers between devices  26.7 us (5%)
  between operations  14.1 us (2%)
  other arithmetic  8.13 us (1%)
  local copies, waits for them, and re-layouts  7.88 us (1%)
    pallas_call x1, Pallas kernels, gather_all(): pl.pallas_call(gather_kernel, out_shape=(jax.ShapeDtypeStruct((7, 256, SC...  218 us
    psum x1, blocking collectives, on_device(): left_sq = lax.psum(jnp.sum(left_prod * left_prod, axis=0), 'row')  123 us
    all_to_all x1, starting transfers between devices, on_device(): lax.all_to_all(lp, 'col', 0, 0, tiled=True).astype(F32)  115 us
    all_gather x1, waiting for transfers between devices, on_device(): left_rows = lax.all_gather(left_half, 'col', axis=1, tiled=True)  26.7 us
    all_to_all x1, starting transfers between devices, on_device(): lax.all_to_all(parts, 'row', 0, 0, tiled=True).astype(F32)  25.4 us
    psum x1, blocking collectives, on_device(): right_sq = lax.psum(jnp.sum(right_prod * right_prod, axis=0), 'col')  19.7 us
    pallas_call x1, Pallas kernels, product(): pl.pallas_call(product_kernel, grid=(7,), out_shape=(jax.ShapeDtypeStruct...  12.8 us
  transfers between devices with their start and end apart: 3, of which 1 were waited for; matrix products, arithmetic and copies ran while one was open for 1% of the time, Pallas kernels for 2%

profile of v1, /device:TPU:1, one launch (start us, length us, event | category | flops | bytes accessed | tf_op | source)
XLA Modules:
  0.0 572.0 jit_solution(8080532064525474332)
XLA Ops:
  7.2 0.0 copy-start.2
  7.2 1.1 copy-done.2
  8.3 0.0 copy-start.3
  8.3 1.0 copy-done.3
  9.3 0.0 copy-start.4
  9.3 0.9 copy-done.4
  10.2 217.6 %gather_gram.1 = (f32[7,256,896]{2,1,0:T(8,128)}, bf16[8,2,448,256]{3,2,1,0:T(8,128)(2,1)}, bf16[64,48,384]{2,1,0:T(8,128)(2,1)S(1)}, bf16[8,192,384]{2,1,0:T(8,128)(2,1)}) custom-call(bf16[4,48,1792]{2,1,0:T(8,128)(2,1)S(1)} %bitcast.8, bf16[4,48,384]{2,1,0:T(8,128)(2,1)S(1)} %bitcast.10, bf16[2,448,256]{2,1,0:T(8,128)(2,1)S(1)} %bitcast.9), custom_call_target="tpu_custom_call" | custom-call | tf_op jit(solution)/shard_map/gather_gram/pallas_call | solution.py:367
  227.8 114.5 %all-to-all-start = ((bf16[8,192,384]{2,1,0:T(8,128)(2,1)}), bf16[8,192,384]{2,1,0:T(8,128)(2,1)S(1)}, u32[]{:S(2)}, u32[]{:S(2)}) async-start(bf16[8,192,384]{2,1,0:T(8,128)(2,1)} %get-tuple-element.10), calls=%async_computation | async-start | bytes 2359296 | tf_op jit(solution)/shard_map/all_to_all | solution.py:428
  342.4 0.0 copy-start
  342.4 2.8 copy-done
  345.2 0.0 copy-start.1
  345.2 2.0 copy-done.1
  347.2 12.8 %product.1 = (f32[1792,896]{1,0:T(8,128)}, bf16[16,1792,128]{2,1,0:T(8,128)(2,1)}) custom-call(f32[7,256,896]{2,1,0:T(8,128)S(1)} %copy-done, f32[1792,896]{1,0:T(8,128)} %factor.1, bf16[8,896,256]{2,1,0:T(8,128)(2,1)S(1)} %bitcast.7), custom_call_target="tpu_custom_call" | custom-call | tf_op jit(solution)/shard_map/product/pallas_call | solution.py:404
  360.1 0.0 all-to-all-done
  360.1 25.4 %all-to-all-start.1 = ((bf16[16,1792,128]{2,1,0:T(8,128)(2,1)}), bf16[16,1792,128]{2,1,0:T(8,128)(2,1)}, u32[]{:S(2)}, u32[]{:S(2)}) async-start(bf16[16,1792,128]{2,1,0:T(8,128)(2,1)} %get-tuple-element.15), calls=%async_computation.1 | async-start | bytes 14680064 | tf_op jit(solution)/shard_map/all_to_all | solution.py:433
  385.4 0.0 all-gather.2.cloned.1.call-start
  385.5 0.2 convert_reduce_fusion.1
  385.7 1.8 fusion
  387.4 0.0 all-gather.2.cloned.1.call-update
  387.5 26.7 %all-gather.2.cloned.1.call-done = bf16[192,3072]{1,0:T(8,128)(2,1)} async-done(((bf16[192,384]{1,0:T(8,128)(2,1)}), bf16[192,3072]{1,0:T(8,128)(2,1)}) %all-gather.2.cloned.1.call-update) | async-done | bytes 1179664 | tf_op jit(solution)/shard_map/all_gather | solution.py:431
  414.1 2.1 multiply_reduce_fusion.1
  416.2 123.1 %psum.14 = f32[384]{0:T(512)S(1)} all-reduce(f32[384]{0:T(512)S(1)} %get-tuple-element.18), channel_id=1, replica_groups=mesh['row'=16,'col'=8] {'row'}, use_global_device_ids=true, to_apply=%region_2.0 | all-reduce | flops 384 | bytes 3072 | tf_op jit(solution)/shard_map/psum | solution.py:434
  539.3 0.7 broadcast_multiply_fusion.1
  540.0 0.0 all-to-all-done.1
  540.0 4.2 convert_reduce_fusion
  544.2 0.3 multiply_reduce_fusion
  544.5 19.7 %psum.15 = f32[128]{0:T(128)S(1)} all-reduce(f32[128]{0:T(128)S(1)} %multiply_reduce_fusion), channel_id=1, replica_groups=mesh['row'=16,'col'=8] {'col'}, use_global_device_ids=true, to_apply=%region_5.0 | all-reduce | flops 128 | bytes 1024 | tf_op jit(solution)/shard_map/psum | solution.py:435
  564.2 1.0 broadcast_multiply_fusion
  (2 shorter events, 0.0 us)
Async XLA Ops:
  7.2 1.1 copy-start.2
  8.3 1.0 copy-start.3
  9.3 0.9 copy-start.4
  227.8 132.2 %all-to-all-start = ((bf16[8,192,384]{2,1,0:T(8,128)(2,1)}), bf16[8,192,384]{2,1,0:T(8,128)(2,1)S(1)}, u32[]{:S(2)}, u32[]{:S(2)}) async-start(bf16[8,192,384]{2,1,0:T(8,128)(2,1)} %get-tuple-element.10), calls=%async_computation | async-start | bytes 2359296 | tf_op jit(solution)/shard_map/all_to_all | solution.py:428
  342.4 2.8 copy-start
  345.2 2.0 copy-start.1
  360.1 180.0 %all-to-all-start.1 = ((bf16[16,1792,128]{2,1,0:T(8,128)(2,1)}), bf16[16,1792,128]{2,1,0:T(8,128)(2,1)}, u32[]{:S(2)}, u32[]{:S(2)}) async-start(bf16[16,1792,128]{2,1,0:T(8,128)(2,1)} %get-tuple-element.15), calls=%async_computation.1 | async-start | bytes 14680064 | tf_op jit(solution)/shard_map/all_to_all | solution.py:433
  385.4 28.7 %all-gather.2.cloned.1.call-start = ((), (), s32[]{:S(2)}) async-start(), calls=%async_computation.2 | async-start | bytes 1327104 | tf_op jit(solution)/shard_map/all_gather | solution.py:431
Sparse Core Ops, SparseCore 0:
  388.5 25.5 all-gather.1

commit v2 on v1

--- a/solution.py
+++ b/solution.py
@@ -19,6 +19,10 @@
 W = GC + LC
 SC = 896
 FIRST, SECOND = "f", "s"
+TILES = ((0, 512), (512, 512), (1024, 512), (1536, 256))
+PIECE = [n // 4 for _, n in TILES]
+PLACE = [0, 128, 256, 384]
+A1, B1, C1, A2, B2, C2 = range(6)
 
 
 def wrap(v):
@@ -56,10 +60,14 @@
 ]
 
 
-def gather_kernel(
-    grad, lbas, rbas, acc_o, bas_o, lb_o, lp_o,
-    slab, shared, acc, bas, lp,
+def kernel(
+    grad, lbas, rbas, rfac, lfac,
+    rnew_o, rprod_o, rsum_o, lnew_o, lprod_o, lsum_o,
+    slab, shared, acc, bas, lp, prod,
+    ra, tb, rb, rc, s1, keep, ra2, tb2, rb2, rc2, rout, rsq,
+    lrecv, lrows, lf, ln, lpr, lsq,
     ag_s, ag_r, y_s, y_r, sib_s, sib_r, loc, bs, br, bss, bsr, cp,
+    rs_s, rs_r, l1s, l1r, l2s, l2r, l3s, l3r, q_s, q_r,
 ):
     row = lax.axis_index("row")
     col = lax.axis_index("col")
@@ -105,16 +113,33 @@
         pltpu.make_async_copy(lbas, slab.at[pl.ds(row * 4, 4), :, pl.ds(GC, LC)], cp.at[1]),
         pltpu.make_async_copy(rbas, bas.at[col], cp.at[2]),
     ]
-    for c in own:
+    late = [
+        pltpu.make_async_copy(rfac, acc, cp.at[3]),
+        pltpu.make_async_copy(lfac, lf, cp.at[4]),
+    ]
+    for c in own + late:
         c.start()
 
+    def colmate(i):
+        return {"col": (col + i) % 8}
+
+    def rowmate(i):
+        return {"row": (row + i) % 16}
+
     barrier = pltpu.get_barrier_semaphore()
-    peers = [neighbour(0, a, d) for a in (FIRST, SECOND) for d in (1, -1)] + [ydev(1), ydev(-1), sib]
-    for peer in peers:
-        pl.semaphore_signal(barrier, inc=1, device_id=peer, device_id_type=MESH)
+
+    def greet(make, n):
+        def body(i, carry):
+            pl.semaphore_signal(barrier, inc=1, device_id=make(i), device_id_type=MESH)
+            return carry
+
+        lax.fori_loop(1, n, body, 0)
+
+    greet(colmate, 8)
+    greet(rowmate, 16)
     for c in own:
         c.wait()
-    pl.semaphore_wait(barrier, len(peers))
+    pl.semaphore_wait(barrier, 22)
 
     is_k = k == z // 2
     role = (y - x + 4) % 4
@@ -162,19 +187,23 @@
                     to_sib(src, h, df, ds).start()
                     local(h, df, ds).start()
 
+    def hop(h):
+        return role if h == 0 else (4 - role) % 4
+
     def relay_units(step):
-        @pl.when(relay)
-        def _():
-            for df, ds in UNITS[step]:
-                for h in (0, 1):
-                    ref = unit_region(h, df, ds)
-                    to_y(ref, h, df, ds).wait_recv()
-
-                    @pl.when(role != last_role(h))
-                    def _():
-                        to_y(ref, h, df, ds).start()
-
-                    to_sib(ref, h, df, ds).start()
+        for hops, lag in ((1, 1), (2, 1), (3, 2)):
+            if not 0 <= step - lag <= 8:
+                continue
+            for h in (0, 1):
+
+                @pl.when(jnp.logical_and(is_k, hop(h) == hops))
+                def _():
+                    for df, ds in UNITS[step - lag]:
+                        ref = unit_region(h, df, ds)
+                        to_y(ref, h, df, ds).wait_recv()
+                        if hops < 3:
+                            to_y(ref, h, df, ds).start()
+                        to_sib(ref, h, df, ds).start()
 
     def b_ref(dy, kk, part):
         c = ((y + dy + 4) % 4) * 2 + kk
@@ -192,8 +221,7 @@
             src_ref=ref, dst_ref=ref, send_sem=bss.at[i], recv_sem=bsr.at[i], device_id=sib, device_id_type=MESH,
         )
 
-    def group(dx, first, last):
-        xg = (x + dx + 4) % 4
+    def group_ready(dx):
         units = [(0, dx, dz) for dz in (-1, 0, 1, 2)] + [(1, dz, dx) for dz in (-1, 0, 1, 2)]
 
         @pl.when(jnp.logical_not(is_k))
@@ -206,6 +234,8 @@
             for u in units:
                 local(*u).wait()
 
+    def gram(dx, first, lo, hi):
+        xg = (x + dx + 4) % 4
         rows = pl.ds(xg * 16, 16)
 
         def tile(m, carry):
@@ -213,24 +243,195 @@
             a = slab[rows, :, cols].reshape(768, 256)
             b = shared[rows].reshape(768, SC)
             d = lax.dot_general(a, b, (((0,), (0,)), ((), ())), preferred_element_type=F32)
+            old = acc[cols, :]
             if first:
-                acc[m] = d
-            else:
-                acc[m] = acc[m] + d
-            if last:
-                pltpu.make_async_copy(acc.at[m], acc_o.at[m], cp.at[m]).start()
+                old = ema_decay * old
+            acc[cols, :] = old + (1.0 - ema_decay) * d
             return carry
 
-        lax.fori_loop(0, 7, tile, 0)
-
-        def left(j, carry):
+        lax.fori_loop(lo, hi, tile, 0)
+
+    def l1(c, mine):
+        return pltpu.make_async_remote_copy(
+            src_ref=lp.at[c], dst_ref=lrecv.at[mine], send_sem=l1s.at[c], recv_sem=l1r.at[mine],
+            device_id={"col": c}, device_id_type=MESH,
+        )
+
+    def left(dx):
+        xg = (x + dx + 4) % 4
+
+        def part(j, carry):
+            c = xg * 2 + j
             a = slab[pl.ds(row * 4, 4), :, pl.ds(0, GC)].reshape(192, GC)
             b = slab[pl.ds(xg * 16 + j * 8, 8), :, pl.ds(0, GC)].reshape(384, GC)
             d = lax.dot_general(a, b, (((1,), (1,)), ((), ())), preferred_element_type=F32)
-            lp[xg * 2 + j] = d.astype(BF16)
+            lp[c] = d.astype(BF16)
+
+            @pl.when(c != col)
+            def _():
+                l1(c, col).start()
+
             return carry
 
-        lax.fori_loop(0, 2, left, 0)
+        lax.fori_loop(0, 2, part, 0)
+
+    def l2(i):
+        return pltpu.make_async_remote_copy(
+            src_ref=lrows.at[col], dst_ref=lrows.at[col], send_sem=l2s.at[i], recv_sem=l2r.at[i],
+            device_id=colmate(i), device_id_type=MESH,
+        )
+
+    def l3(i):
+        return pltpu.make_async_remote_copy(
+            src_ref=lsq.at[row], dst_ref=lsq.at[row], send_sem=l3s.at[i], recv_sem=l3r.at[i],
+            device_id=rowmate(i), device_id_type=MESH,
+        )
+
+    def rq(i):
+        return pltpu.make_async_remote_copy(
+            src_ref=rsq.at[col], dst_ref=rsq.at[col], send_sem=q_s.at[i], recv_sem=q_r.at[i],
+            device_id=colmate(i), device_id_type=MESH,
+        )
+
+    def each(n, make, what):
+        def body(i, carry):
+            c = make(i)
+            getattr(c, what)()
+            return carry
+
+        lax.fori_loop(1, n, body, 0)
+
+    def left_refresh():
+        total = lp[col].astype(F32)
+        for i in range(1, 8):
+            c = (col + i) % 8
+            l1(c, c).wait_recv()
+            total = total + lrecv[c].astype(F32)
+        new = ema_decay * lf[...] + (1.0 - ema_decay) * total
+        ln[...] = new
+        lrows[col] = new.astype(BF16)
+        each(8, l2, "start")
+        pltpu.make_async_copy(ln, lnew_o, cp.at[5]).start()
+
+    def left_product():
+        each(8, l2, "wait_recv")
+
+        def part(c, carry):
+            b = slab[pl.ds(c * 8, 8), :, pl.ds(GC, LC)].reshape(384, LC)
+            return carry + jnp.dot(lrows[c], b, preferred_element_type=F32)
+
+        lpr[...] = lax.fori_loop(0, 8, part, jnp.zeros((192, LC), F32))
+        v = lpr[...]
+        lsq[row] = jnp.broadcast_to(jnp.sum(v * v, axis=0, keepdims=True), (8, LC))
+        each(16, l3, "start")
+        pltpu.make_async_copy(lpr, lprod_o, cp.at[6]).start()
+
+    def make_product(t):
+        lo, n = TILES[t]
+        pltpu.make_async_copy(acc.at[pl.ds(lo, n)], rnew_o.at[pl.ds(lo, n)], cp.at[8 + t]).start()
+
+        def part(i, carry):
+            c, r = i // 2, i % 2
+            start = pl.multiple_of(lo + r * (n // 2), 128)
+            half = acc[pl.ds(start, n // 2), :].astype(BF16)
+            d = jnp.dot(half, bas[c].reshape(SC, 256), preferred_element_type=F32).astype(BF16)
+            xo, zo = c // 2, (c % 2) * 2
+            prod[xo, zo, pl.ds(start, n // 2), :] = d[:, :128]
+            prod[xo, zo + 1, pl.ds(start, n // 2), :] = d[:, 128:]
+            return carry
+
+        lax.fori_loop(0, 16, part, 0)
+
+    TYPES = (0, 1, 2, 3)
+
+    def hd(i):
+        return i // 2, 1 if i % 2 == 0 else -1
+
+    def rows_of(i, t):
+        return pl.ds(TILES[t][0] + i * PIECE[t], PIECE[t])
+
+    def spot(t):
+        return pl.ds(PLACE[t], PIECE[t])
+
+    def pos(h, axis):
+        return x if (h == 0) == (axis == FIRST) else z
+
+    def chunk(i, t, e):
+        h, _ = hd(i)
+        p = (pos(h, FIRST) + e + 4) % 4
+        return prod.at[p, :, rows_of(i, t), :] if h == 0 else prod.at[:, p, rows_of(i, t), :]
+
+    def rs(kind, i, t):
+        h, d = hd(i)
+        axis = FIRST if kind < A2 else SECOND
+        q = (pos(h, SECOND) + 4) % 4
+        if kind == A1:
+            src, dst, to = chunk(i, t, 2), ra.at[i, :, spot(t), :], d
+        elif kind == B1:
+            src, dst, to = tb.at[i, :, spot(t), :], rb.at[i, :, spot(t), :], d
+        elif kind == C1:
+            src, dst, to = chunk(i, t, -d), rc.at[i, :, spot(t), :], -d
+        elif kind == A2:
+            src, dst, to = s1.at[i, (q + 2) % 4, spot(t), :], ra2.at[i, spot(t), :], d
+        elif kind == B2:
+            src, dst, to = tb2.at[i, spot(t), :], rb2.at[i, spot(t), :], d
+        else:
+            src, dst, to = s1.at[i, (q - d + 4) % 4, spot(t), :], rc2.at[i, spot(t), :], -d
+        return pltpu.make_async_remote_copy(
+            src_ref=src, dst_ref=dst, send_sem=rs_s.at[kind, i * 4 + t], recv_sem=rs_r.at[kind, i * 4 + t],
+            device_id=neighbour(h, axis, to), device_id_type=MESH,
+        )
+
+    def r0(t):
+        for kind in (A1, C1):
+            for i in TYPES:
+                rs(kind, i, t).start()
+
+    def r1(t):
+        for i in TYPES:
+            h, d = hd(i)
+            rs(A1, i, t).wait_recv()
+            mine = chunk(i, t, d)
+            tb[i, :, spot(t), :] = (mine[...].astype(F32) + ra[i, :, spot(t), :].astype(F32)).astype(BF16)
+            rs(B1, i, t).start()
+
+    def r2(t):
+        for i in TYPES:
+            h, d = hd(i)
+            rs(C1, i, t).wait_recv()
+            rs(B1, i, t).wait_recv()
+            mine = chunk(i, t, 0)
+            q = pos(h, SECOND)
+
+            s1[i, :, spot(t), :] = (
+                mine[...].astype(F32) + rb[i, :, spot(t), :].astype(F32) + rc[i, :, spot(t), :].astype(F32)
+            ).astype(BF16)
+            rs(A2, i, t).start()
+            rs(C2, i, t).start()
+            own_chunk = prod.at[x, z, rows_of(i, t), :]
+            keep[i, spot(t), :] = (
+                own_chunk[...].astype(F32) + rb[i, q, spot(t), :].astype(F32) + rc[i, q, spot(t), :].astype(F32)
+            )
+
+    def r3(t):
+        for i in TYPES:
+            h, d = hd(i)
+            q = (pos(h, SECOND) + d + 4) % 4
+            rs(A2, i, t).wait_recv()
+            tb2[i, spot(t), :] = (s1[i, q, spot(t), :].astype(F32) + ra2[i, spot(t), :].astype(F32)).astype(BF16)
+            rs(B2, i, t).start()
+
+    def r4(t):
+        total = jnp.zeros((8, 128), F32)
+        for i in TYPES:
+            rs(C2, i, t).wait_recv()
+            rs(B2, i, t).wait_recv()
+            v = keep[i, spot(t), :] + rb2[i, spot(t), :].astype(F32) + rc2[i, spot(t), :].astype(F32)
+            rout[rows_of(i, t), :] = v
+            total = total + jnp.sum((v * v).reshape(PIECE[t] // 8, 8, 128), axis=0)
+        lo, n = TILES[t]
+        pltpu.make_async_copy(rout.at[pl.ds(lo, n)], rprod_o.at[pl.ds(lo, n)], cp.at[12 + t]).start()
+        return total
 
     sent = []
 
@@ -260,7 +461,7 @@
             for d in (1, -1):
                 go(h, df, 0, "full", SECOND, d)
     source_units(1)
-    relay_units(0)
+    relay_units(1)
     for h in H:
         ag_wait(h, 0, -1, "full", SECOND, 1)
         ag_wait(h, 0, 1, "full", SECOND, -1)
@@ -268,7 +469,7 @@
         go(h, 0, -1, 0, SECOND, 1)
         go(h, 0, 1, 1, SECOND, -1)
     source_units(2)
-    relay_units(1)
+    relay_units(2)
     b_send(0, -1, "full", 1).wait_recv()
     b_send(1, 1, "full", -1).wait_recv()
     more = [b_send(2, -1, 0, 1), b_send(3, 1, 1, -1)]
@@ -284,7 +485,7 @@
         for d in (1, -1):
             go(h, 2, 0, "full", SECOND, d)
     source_units(3)
-    relay_units(2)
+    relay_units(3)
     for df in (-1, 1):
         for h in H:
             ag_wait(h, df, -1, "full", SECOND, 1)
@@ -294,7 +495,7 @@
             go(h, df, -1, 0, SECOND, 1)
             go(h, df, 1, 1, SECOND, -1)
     source_units(4)
-    relay_units(3)
+    relay_units(4)
     b_send(2, 2, 0, 1).wait_recv()
     b_send(3, 2, 1, -1).wait_recv()
     c = b_sib(3, 2, k)
@@ -304,7 +505,7 @@
         ag_wait(h, 0, 2, 0, SECOND, 1)
         ag_wait(h, 0, 2, 1, SECOND, -1)
     source_units(5)
-    relay_units(4)
+    relay_units(5)
     for h in H:
         ag_wait(h, 2, -1, "full", SECOND, 1)
         ag_wait(h, 2, 1, "full", SECOND, -1)
@@ -312,31 +513,74 @@
         go(h, 2, -1, 0, SECOND, 1)
         go(h, 2, 1, 1, SECOND, -1)
     source_units(6)
-    relay_units(5)
-    group(0, True, False)
+    relay_units(6)
     for df in (-1, 1):
         for h in H:
             ag_wait(h, df, 2, 0, SECOND, 1)
             ag_wait(h, df, 2, 1, SECOND, -1)
     source_units(7)
-    relay_units(6)
+    relay_units(7)
+    late[0].wait()
+    group_ready(0)
+    gram(0, True, 0, 7)
+    left(0)
     for h in H:
         ag_wait(h, 2, 2, 0, SECOND, 1)
         ag_wait(h, 2, 2, 1, SECOND, -1)
     source_units(8)
-    lb_copy = pltpu.make_async_copy(slab.at[:, :, pl.ds(GC, LC)], lb_o, cp.at[7])
-    lb_copy.start()
-    relay_units(7)
-    group(-1, False, False)
     relay_units(8)
+    relay_units(9)
+    group_ready(-1)
+    gram(-1, False, 0, 7)
+    left(-1)
+    relay_units(10)
+    group_ready(1)
+    gram(1, False, 0, 7)
+    left(1)
     for i, dy in enumerate((0, -1, 1, 2)):
         b_sib(i, dy, 1 - k).wait_recv()
-    bas_copy = pltpu.make_async_copy(bas, bas_o, cp.at[8])
-    bas_copy.start()
-    group(1, False, False)
-    group(2, False, True)
-    lp_copy = pltpu.make_async_copy(lp, lp_o, cp.at[9])
-    lp_copy.start()
+    group_ready(2)
+    gram(2, False, 0, 2)
+    make_product(0)
+    r0(0)
+    gram(2, False, 2, 4)
+    make_product(1)
+    r0(1)
+    r1(0)
+    gram(2, False, 4, 6)
+    make_product(2)
+    r0(2)
+    r1(1)
+    gram(2, False, 6, 7)
+    make_product(3)
+    r0(3)
+    left(2)
+    r1(2)
+    r2(0)
+    late[1].wait()
+    r1(3)
+    r3(0)
+    r2(1)
+    left_refresh()
+    total = r4(0)
+    r3(1)
+    r2(2)
+    total = total + r4(1)
+    r3(2)
+    left_product()
+    r2(3)
+    total = total + r4(2)
+    r3(3)
+    total = total + r4(3)
+    rsq[col] = total
+    each(8, rq, "start")
+
+    each(16, l3, "wait_recv")
+    lsum = pltpu.make_async_copy(lsq, lsum_o, cp.at[7])
+    lsum.start()
+    each(8, rq, "wait_recv")
+    rsum = pltpu.make_async_copy(rsq, rsum_o, cp.at[16])
+    rsum.start()
 
     for c in sent + b_sends + b_sibs:
         c.wait_send()
@@ -345,7 +589,7 @@
             for h in H:
                 ref = unit_region(h, df, ds)
 
-                @pl.when(jnp.logical_and(is_k, jnp.logical_or(role == 0, role != last_role(h))))
+                @pl.when(jnp.logical_and(is_k, hop(h) != 3))
                 def _():
                     to_y(ref, h, df, ds).wait_send()
 
@@ -353,86 +597,71 @@
                 def _():
                     to_sib(ref, h, df, ds).wait_send()
 
-    for m in range(7):
-        pltpu.make_async_copy(acc.at[m], acc_o.at[m], cp.at[m]).wait()
-    lb_copy.wait()
-    bas_copy.wait()
-    lp_copy.wait()
-
-
-def gather_all(gradient, left_basis, right_basis):
+    for kind in range(6):
+        for i in TYPES:
+            for t in range(4):
+                rs(kind, i, t).wait_send()
+    for i in range(1, 8):
+        l1((col + i) % 8, col).wait_send()
+    each(8, l2, "wait_send")
+    each(16, l3, "wait_send")
+    each(8, rq, "wait_send")
+    for t, (lo, n) in enumerate(TILES):
+        pltpu.make_async_copy(acc.at[pl.ds(lo, n)], rnew_o.at[pl.ds(lo, n)], cp.at[8 + t]).wait()
+        pltpu.make_async_copy(rout.at[pl.ds(lo, n)], rprod_o.at[pl.ds(lo, n)], cp.at[12 + t]).wait()
+    pltpu.make_async_copy(ln, lnew_o, cp.at[5]).wait()
+    pltpu.make_async_copy(lpr, lprod_o, cp.at[6]).wait()
+    lsum.wait()
+    rsum.wait()
+
+
+def refresh(gradient, left_basis, right_basis, right_factor, left_factor):
     dma = pltpu.SemaphoreType.DMA
     n = len(AG)
     any_spec = pl.BlockSpec(memory_space=pl.ANY)
+    V = pltpu.VMEM
     return pl.pallas_call(
-        gather_kernel,
+        kernel,
         out_shape=(
-            jax.ShapeDtypeStruct((7, 256, SC), F32),
-            jax.ShapeDtypeStruct((8, 2, 448, 256), BF16),
-            jax.ShapeDtypeStruct((64, 48, LC), BF16),
-            jax.ShapeDtypeStruct((8, 192, LC), BF16),
+            jax.ShapeDtypeStruct((GC, SC), F32),
+            jax.ShapeDtypeStruct((GC, 128), F32),
+            jax.ShapeDtypeStruct((8, 8, 128), F32),
+            jax.ShapeDtypeStruct((192, LC), F32),
+            jax.ShapeDtypeStruct((192, LC), F32),
+            jax.ShapeDtypeStruct((16, 8, LC), F32),
         ),
-        in_specs=[any_spec] * 3,
-        out_specs=[any_spec] * 4,
+        in_specs=[any_spec] * 5,
+        out_specs=[any_spec] * 6,
         scratch_shapes=[
-            pltpu.VMEM((64, 48, W), BF16),
-            pltpu.VMEM((64, 48, SC), BF16),
-            pltpu.VMEM((7, 256, SC), F32),
-            pltpu.VMEM((8, 2, 448, 256), BF16),
-            pltpu.VMEM((8, 192, LC), BF16),
+            V((64, 48, W), BF16), V((64, 48, SC), BF16), V((GC, SC), F32), V((8, 2, 448, 256), BF16),
+            V((8, 192, LC), BF16), V((4, 4, GC, 128), BF16),
+            V((4, 4, 448, 128), BF16), V((4, 4, 448, 128), BF16), V((4, 4, 448, 128), BF16),
+            V((4, 4, 448, 128), BF16), V((4, 4, 448, 128), BF16), V((4, 448, 128), F32),
+            V((4, 448, 128), BF16), V((4, 448, 128), BF16), V((4, 448, 128), BF16), V((4, 448, 128), BF16),
+            V((GC, 128), F32), V((8, 8, 128), F32),
+            V((8, 192, LC), BF16), V((8, 192, LC), BF16), V((192, LC), F32), V((192, LC), F32), V((192, LC), F32),
+            V((16, 8, LC), F32),
             dma((n,)), dma((n,)), dma((32,)), dma((32,)), dma((32,)), dma((32,)), dma((32,)),
-            dma((4,)), dma((4,)), dma((4,)), dma((4,)), dma((10,)),
+            dma((4,)), dma((4,)), dma((4,)), dma((4,)), dma((17,)),
+            dma((6, 16)), dma((6, 16)), dma((8,)), dma((8,)), dma((8,)), dma((8,)), dma((16,)), dma((16,)),
+            dma((8,)), dma((8,)),
         ],
         compiler_params=pltpu.CompilerParams(
-            collective_id=0, has_side_effects=True, vmem_limit_bytes=48 * 1024 * 1024
+            collective_id=0, has_side_effects=True, vmem_limit_bytes=67043328
         ),
-        name="gather_gram",
-    )(gradient.reshape(4, 48, GC), left_basis.reshape(4, 48, LC), right_basis.reshape(2, 448, 256))
-
-
-def product_kernel(acc, factor, basis, new, part):
-    value = ema_decay * factor[...] + (1.0 - ema_decay) * acc[0]
-    new[...] = value
-    half = value.astype(BF16)
-    for c in range(8):
-        d = jnp.dot(half, basis[c], preferred_element_type=F32).astype(BF16)
-        part[2 * c] = d[:, :128]
-        part[2 * c + 1] = d[:, 128:]
-
-
-def product(acc, factor, basis):
-    return pl.pallas_call(
-        product_kernel,
-        grid=(7,),
-        out_shape=(
-            jax.ShapeDtypeStruct((GC, SC), F32),
-            jax.ShapeDtypeStruct((16, GC, 128), BF16),
-        ),
-        in_specs=[
-            pl.BlockSpec((1, 256, SC), lambda i: (i, 0, 0)),
-            pl.BlockSpec((256, SC), lambda i: (i, 0)),
-            pl.BlockSpec((8, SC, 256), lambda i: (0, 0, 0)),
-        ],
-        out_specs=(
-            pl.BlockSpec((256, SC), lambda i: (i, 0)),
-            pl.BlockSpec((16, 256, 128), lambda i: (0, i, 0)),
-        ),
-        compiler_params=pltpu.CompilerParams(vmem_limit_bytes=40 * 1024 * 1024),
-        name="product",
-    )(acc, factor, basis)
+        name="refresh",
+    )(
+        gradient.reshape(4, 48, GC), left_basis.reshape(4, 48, LC), right_basis.reshape(2, 448, 256),
+        right_factor, left_factor,
+    )
 
 
 def on_device(gradient, left_factor, right_factor, left_basis, right_basis):
-    acc, basis, lb, lp = gather_all(gradient, left_basis, right_basis)
-    right_new, parts = product(acc, right_factor, basis.reshape(8, SC, 256))
-    gram_block = jnp.sum(lax.all_to_all(lp, "col", 0, 0, tiled=True).astype(F32), axis=0)
-    left_new = ema_decay * left_factor + (1.0 - ema_decay) * gram_block
-    left_half = left_new.astype(BF16)
-    left_rows = lax.all_gather(left_half, "col", axis=1, tiled=True)
-    left_prod = jnp.dot(left_rows, lb.reshape(DMODEL, LC), preferred_element_type=F32)
-    right_prod = jnp.sum(lax.all_to_all(parts, "row", 0, 0, tiled=True).astype(F32), axis=0)
-    left_sq = lax.psum(jnp.sum(left_prod * left_prod, axis=0), "row")
-    right_sq = lax.psum(jnp.sum(right_prod * right_prod, axis=0), "col")
+    right_new, right_prod, rsq, left_new, left_prod, lsq = refresh(
+        gradient, left_basis, right_basis, right_factor, left_factor
+    )
+    left_sq = jnp.sum(lsq[:, 0], axis=0)
+    right_sq = jnp.sum(rsq, axis=(0, 1))
     left_out = left_prod * lax.rsqrt(left_sq / DMODEL + epsilon)
     right_out = right_prod * lax.rsqrt(right_sq / DHIDDEN + epsilon)
     return (left_new, right_new, left_out, right_out)

time: 573 us -> 192 us (0.34)
  blocking collectives: 143 us -> 0 us
  starting transfers between devices: 140 us -> 0 us
  Pallas kernels: 230 us -> 178 us
  waiting for transfers between devices: 26.7 us -> 0 us
  between operations: 14.1 us -> 0.65 us
    psum x2 -> x0, blocking collectives: 143 us -> none  [the longest x1 123 us: on_device(): left_sq = lax.psum(jnp.sum(left_prod * left_prod, axis=0), 'row')]
    all_to_all x2 -> x0, starting transfers between devices: 140 us -> none  [the longest x1 115 us: on_device(): lax.all_to_all(lp, 'col', 0, 0, tiled=True).astype(F32)]
    pallas_call x2 -> x1, Pallas kernels: 230 us -> 178 us  [refresh(): pl.pallas_call(kernel, out_shape=(jax.ShapeDtypeStruct((GC, SC), F32), ja...]
    all_gather x1 -> x0, waiting for transfers between devices: 26.7 us -> none  [on_device(): left_rows = lax.all_gather(left_half, 'col', axis=1, tiled=True)]
  transfers between devices with their start and end apart: 3 -> 0, of which waited for: 1 -> 0; matrix products, arithmetic and copies ran while one was open for 1% -> 0% of each run, Pallas kernels for 2% -> 0%
where the time goes in v2:
time: 192 us
  Pallas kernels  178 us (93%)
  local copies, waits for them, and re-layouts  7.67 us (4%)
  other arithmetic  5.62 us (3%)
    pallas_call x1, Pallas kernels, refresh(): pl.pallas_call(kernel, out_shape=(jax.ShapeDtypeStruct((GC, SC), F32), ja...  178 us
    unnamed x2, local copies, waits for them, and re-layouts  7.67 us

profile of v2, /device:TPU:1, one launch (start us, length us, event | category | flops | bytes accessed | tf_op | source)
XLA Modules:
  0.0 191.8 jit_solution(13400307974293070949)
XLA Ops:
  0.6 177.9 %refresh.1 = (f32[1792,896]{1,0:T(8,128)}, f32[1792,128]{1,0:T(8,128)}, f32[8,8,128]{2,1,0:T(8,128)}, f32[192,384]{1,0:T(8,128)}, f32[192,384]{1,0:T(8,128)}, /*index=5*/f32[16,8,384]{2,1,0:T(8,128)}) custom-call(bf16[4,48,1792]{2,1,0:T(8,128)(2,1)} %bitcast.3, bf16[4,48,384]{2,1,0:T(8,128)(2,1)} %bitcast.5, bf16[2,448,256]{2,1,0:T(8,128)(2,1)} %bitcast.4, ...), custom_call_target="tpu_custom_call" | custom-call | tf_op jit(solution)/shard_map/refresh/pallas_call | solution.py:623
  178.5 0.8 reduce_sum.19
  179.3 2.2 %broadcast_multiply_fusion = f32[1792,128]{1,0:T(8,128)} fusion(f32[1792,128]{1,0:T(8,128)} %get-tuple-element.14, f32[128]{0:T(128)S(1)} %add_rsqrt_fusion.1), kind=kLoop, calls=%fused_computation | loop fusion | flops 229376 | bytes 1835520 | tf_op jit(solution)/shard_map/mul | solution.py:666
  181.5 1.0 slice_reduce_fusion
  182.4 1.7 broadcast_multiply_fusion.1
  184.1 1.7 copy.11
  185.8 6.0 %copy.12 = f32[1792,896]{1,0:T(8,128)} copy(f32[1792,896]{1,0:T(8,128)} %get-tuple-element.21) | data formatting | bytes 12845056
  (2 shorter events, 0.0 us)

commit v3 on v2

v3 whole, which is shorter than its diff:
```python
import functools

import jax
import jax.numpy as jnp
from jax import lax
from jax.experimental import pallas as pl
from jax.experimental.pallas import tpu as pltpu
from jax.sharding import PartitionSpec as P

DMODEL = 3072
DHIDDEN = 14336
ema_decay = 0.95
epsilon = 1e-06
MESH = pl.DeviceIdType.MESH
F32 = jnp.float32
BF16 = jnp.bfloat16
GC = 1792
LC = 384
SC = 896
FIRST, SECOND = "f", "s"
TILES = ((0, 512), (512, 512), (1024, 512), (1536, 256))
PIECE = [n // 4 for _, n in TILES]
PLACE = [0, 128, 256, 384]
A1, B1, C1, A2, B2, C2 = range(6)


def wrap(v):
    return (v + 1) % 4 - 1


def message_table():
    keys = []
    for h in (0, 1):
        for axis in (FIRST, SECOND):
            for d in (1, -1):
                keys.append((h, 0, 0, "full", axis, d))
        keys.append((h, -1, 0, 0, FIRST, 1))
        keys.append((h, 1, 0, 1, FIRST, -1))
        for df in (-1, 1, 2):
            for d in (1, -1):
                keys.append((h, df, 0, "full", SECOND, d))
        for df in (0, -1, 1, 2):
            keys.append((h, df, -1, 0, SECOND, 1))
            keys.append((h, df, 1, 1, SECOND, -1))
    return {key: i for i, key in enumerate(keys)}


AG = message_table()
UNITS = [
    (0, 0), (-1, 0), (1, 0), (0, -1), (0, 1), (2, 0), (-1, -1), (-1, 1), (1, -1), (1, 1),
    (0, 2), (2, -1), (2, 1), (-1, 2), (1, 2), (2, 2),
]
LAGS = (1, 2, 4)


def kernel(
    grad, lbas, rbas, rfac, lfac,
    rnew_o, rprod_o, rsum_o, lnew_o, lprod_o, lsum_o,
    slab, lbuf, shared, acc, bas, lp, away, near, both, whole,
    ra, tb, rb, rc, s1, keep, ra2, tb2, rb2, rc2, rout, rsq,
    lsib, lmid, lrecv, lrows, lf, ln, lpr, lsq,
    ag_s, ag_r, lg_s, lg_r, y_s, y_r, sib_s, sib_r, loc, bs, br, bss, bsr, cp,
    rs_s, rs_r, l0s, l0r, l1s, l1r, l2s, l2r, l4s, l4r, l3s, l3r, q_s, q_r,
):
    row = lax.axis_index("row")
    col = lax.axis_index("col")
    x, z = row // 4, row % 4
    y, k = col // 2, col % 2
    sib = {"col": y * 2 + (1 - k)}

    def ydev(d):
        return {"col": ((y + d + 4) % 4) * 2 + k}

    def rid(dx, dz):
        return ((x + dx + 4) % 4) * 4 + (z + dz + 4) % 4

    def region(ref, h, df, ds, part):
        dx, dz = (df, ds) if h == 0 else (ds, df)
        q, n = (0, 2) if part == "full" else (part, 1)
        return ref.at[pl.ds(rid(dx, dz) * 4 + 2 * h + q, n)]

    def neighbour(h, axis, d):
        if (h == 0) == (axis == FIRST):
            return {"row": ((x + d + 4) % 4) * 4 + z}
        return {"row": x * 4 + (z + d + 4) % 4}

    def ag(buf, ss, rr, h, df, ds, part, axis, d, arriving=False):
        if not arriving:
            key = (h, df, ds, part, axis, d)
        elif axis == FIRST:
            key = (h, wrap(df + d), ds, part, axis, d)
        else:
            key = (h, df, wrap(ds + d), part, axis, d)
        i = AG[key]
        ref = region(buf, h, df, ds, part)
        return pltpu.make_async_remote_copy(
            src_ref=ref, dst_ref=ref, send_sem=ss.at[i], recv_sem=rr.at[i],
            device_id=neighbour(h, axis, d), device_id_type=MESH,
        )

    def arrive(net, u):
        df, ds = UNITS[u]
        if u == 0:
            return
        axis = FIRST if ds == 0 else SECOND
        e = df if ds == 0 else ds
        for h in (0, 1):
            if e == 2:
                ag(*net, h, df, ds, 0, axis, 1, True).wait_recv()
                ag(*net, h, df, ds, 1, axis, -1, True).wait_recv()
            else:
                ag(*net, h, df, ds, "full", axis, -e, True).wait_recv()

    def onward(net, u):
        df, ds = UNITS[u]
        out = []
        if u == 0:
            for axis in (FIRST, SECOND):
                for h in (0, 1):
                    for d in (1, -1):
                        out.append((h, 0, 0, "full", axis, d))
        elif ds == 0:
            for h in (0, 1):
                if df == -1:
                    out.append((h, df, 0, 0, FIRST, 1))
                if df == 1:
                    out.append((h, df, 0, 1, FIRST, -1))
            for h in (0, 1):
                for d in (1, -1):
                    out.append((h, df, 0, "full", SECOND, d))
        elif ds != 2:
            for h in (0, 1):
                out.append((h, df, ds, 0 if ds == -1 else 1, SECOND, -ds))
        for key in out:
            c = ag(*net, *key)
            c.start()
            sent.append(c)

    sent = []
    G = (slab, ag_s, ag_r)
    L = (lbuf, lg_s, lg_r)

    own = [
        pltpu.make_async_copy(grad, slab.at[pl.ds(row * 4, 4)], cp.at[0]),
        pltpu.make_async_copy(lbas, lbuf.at[pl.ds(row * 4, 4)], cp.at[1]),
        pltpu.make_async_copy(rbas, bas.at[col], cp.at[2]),
    ]
    late = [
        pltpu.make_async_copy(rfac, acc, cp.at[3]),
        pltpu.make_async_copy(lfac, lf, cp.at[4]),
    ]
    for c in own + late:
        c.start()

    def colmate(i):
        return {"col": (col + i) % 8}

    def rowmate(i):
        return {"row": (row + i) % 16}

    barrier = pltpu.get_barrier_semaphore()

    def greet(make, n):
        def body(i, carry):
            pl.semaphore_signal(barrier, inc=1, device_id=make(i), device_id_type=MESH)
            return carry

        lax.fori_loop(1, n, body, 0)

    greet(colmate, 8)
    greet(rowmate, 16)
    for c in own:
        c.wait()
    pl.semaphore_wait(barrier, 22)

    is_k = k == z // 2
    role = (y - x + 4) % 4
    source = jnp.logical_and(is_k, role == 0)
    relay = jnp.logical_and(is_k, role != 0)
    c0 = pl.multiple_of((z % 2) * SC, 128)

    def unit_id(h, df, ds):
        return h * 16 + (df + 1) * 4 + ds + 1

    def unit_region(h, df, ds):
        return region(shared, h, df, ds, "full")

    def unit_src(h, df, ds):
        dx, dz = (df, ds) if h == 0 else (ds, df)
        return slab.at[pl.ds(rid(dx, dz) * 4 + 2 * h, 2), :, pl.ds(c0, SC)]

    def to_y(src, h, df, ds):
        i = unit_id(h, df, ds)
        return pltpu.make_async_remote_copy(
            src_ref=src, dst_ref=unit_region(h, df, ds), send_sem=y_s.at[i], recv_sem=y_r.at[i],
            device_id=ydev(1 if h == 0 else -1), device_id_type=MESH,
        )

    def to_sib(src, h, df, ds):
        i = unit_id(h, df, ds)
        return pltpu.make_async_remote_copy(
            src_ref=src, dst_ref=unit_region(h, df, ds), send_sem=sib_s.at[i], recv_sem=sib_r.at[i],
            device_id=sib, device_id_type=MESH,
        )

    def local(h, df, ds):
        return pltpu.make_async_copy(unit_src(h, df, ds), unit_region(h, df, ds), loc.at[unit_id(h, df, ds)])

    def last_role(h):
        return 3 if h == 0 else 1

    def source_unit(u):
        @pl.when(source)
        def _():
            df, ds = UNITS[u]
            for h in (0, 1):
                src = unit_src(h, df, ds)
                to_y(src, h, df, ds).start()
                to_sib(src, h, df, ds).start()
                local(h, df, ds).start()

    def hop(h):
        return role if h == 0 else (4 - role) % 4

    def relay_unit(hops, u):
        df, ds = UNITS[u]
        for h in (0, 1):

            @pl.when(jnp.logical_and(is_k, hop(h) == hops))
            def _():
                ref = unit_region(h, df, ds)
                to_y(ref, h, df, ds).wait_recv()
                if hops < 3:
                    to_y(ref, h, df, ds).start()
                to_sib(ref, h, df, ds).start()

    relayed = [0, 0, 0]

    def relay_to(hops, n):
        while relayed[hops - 1] < n:
            relay_unit(hops, relayed[hops - 1])
            relayed[hops - 1] += 1

    def b_ref(dy, kk, part):
        c = ((y + dy + 4) % 4) * 2 + kk
        return bas.at[c] if part == "full" else bas.at[c, part]

    def b_send(i, dy, part, d):
        ref = b_ref(dy, k, part)
        return pltpu.make_async_remote_copy(
            src_ref=ref, dst_ref=ref, send_sem=bs.at[i], recv_sem=br.at[i], device_id=ydev(d), device_id_type=MESH,
        )

    def b_sib(i, dy, kk):
        ref = b_ref(dy, kk, "full")
        return pltpu.make_async_remote_copy(
            src_ref=ref, dst_ref=ref, send_sem=bss.at[i], recv_sem=bsr.at[i], device_id=sib, device_id_type=MESH,
        )

    def group_ready(dx):
        units = [(0, dx, dz) for dz in (-1, 0, 1, 2)] + [(1, dz, dx) for dz in (-1, 0, 1, 2)]

        @pl.when(jnp.logical_not(is_k))
        def _():
            for u in units:
                to_sib(unit_region(*u), *u).wait_recv()

        @pl.when(source)
        def _():
            for u in units:
                local(*u).wait()

    def gram(dx, first, lo, hi):
        xg = (x + dx + 4) % 4
        rows = pl.ds(xg * 16, 16)

        def tile(m, carry):
            cols = pl.ds(pl.multiple_of(m * 256, 256), 256)
            a = slab[rows, :, cols].reshape(768, 256)
            b = shared[rows].reshape(768, SC)
            d = lax.dot_general(a, b, (((0,), (0,)), ((), ())), preferred_element_type=F32)
            old = acc[cols, :]
            if first:
                old = ema_decay * old
            acc[cols, :] = old + (1.0 - ema_decay) * d
            return carry

        lax.fori_loop(lo, hi, tile, 0)

    def l0(yy, c):
        return pltpu.make_async_remote_copy(
            src_ref=lp.at[c], dst_ref=lsib.at[yy], send_sem=l0s.at[yy], recv_sem=l0r.at[yy],
            device_id=sib, device_id_type=MESH,
        )

    def left(dx):
        xg = (x + dx + 4) % 4

        def part(j, carry):
            c = xg * 2 + j
            a = slab[pl.ds(row * 4, 4)].reshape(192, GC)
            b = slab[pl.ds(xg * 16 + j * 8, 8)].reshape(384, GC)
            d = lax.dot_general(a, b, (((1,), (1,)), ((), ())), preferred_element_type=F32)
            lp[c] = d.astype(BF16)

            @pl.when(j != k)
            def _():
                l0(xg, c).start()

            return carry

        lax.fori_loop(0, 2, part, 0)

    def l1(dy):
        yy = (y + dy) % 4
        return pltpu.make_async_remote_copy(
            src_ref=lmid.at[yy], dst_ref=lrecv.at[y], send_sem=l1s.at[dy], recv_sem=l1r.at[dy],
            device_id={"col": yy * 2 + k}, device_id_type=MESH,
        )

    def l2(dy):
        return pltpu.make_async_remote_copy(
            src_ref=lrows.at[col], dst_ref=lrows.at[col], send_sem=l2s.at[dy], recv_sem=l2r.at[dy],
            device_id={"col": ((y + dy) % 4) * 2 + k}, device_id_type=MESH,
        )

    def l4(yy, kk):
        c = yy * 2 + kk
        return pltpu.make_async_remote_copy(
            src_ref=lrows.at[c], dst_ref=lrows.at[c], send_sem=l4s.at[yy], recv_sem=l4r.at[yy],
            device_id=sib, device_id_type=MESH,
        )

    def l3(i):
        return pltpu.make_async_remote_copy(
            src_ref=lsq.at[row], dst_ref=lsq.at[row], send_sem=l3s.at[i], recv_sem=l3r.at[i],
            device_id=rowmate(i), device_id_type=MESH,
        )

    def rq(i):
        return pltpu.make_async_remote_copy(
            src_ref=rsq.at[col], dst_ref=rsq.at[col], send_sem=q_s.at[i], recv_sem=q_r.at[i],
            device_id=colmate(i), device_id_type=MESH,
        )

    def each(n, make, what):
        def body(i, carry):
            c = make(i)
            getattr(c, what)()
            return carry

        lax.fori_loop(1, n, body, 0)

    def left_join():
        for dy in (1, 3, 2):
            yy = (y + dy) % 4
            l0(yy, yy * 2 + k).wait_recv()
            lmid[yy] = (lp[yy * 2 + k].astype(F32) + lsib[yy].astype(F32)).astype(BF16)
            l1(dy).start()

    def left_refresh():
        l0(y, col).wait_recv()
        total = lp[col].astype(F32) + lsib[y].astype(F32)
        for dy in (1, 3, 2):
            l1(dy).wait_recv()
            total = total + lrecv[(y + 4 - dy) % 4].astype(F32)
        new = ema_decay * lf[...] + (1.0 - ema_decay) * total
        ln[...] = new
        lrows[col] = new.astype(BF16)
        for dy in (1, 3, 2):
            l2(dy).start()
        l4(y, k).start()
        pltpu.make_async_copy(ln, lnew_o, cp.at[5]).start()

    def left_share():
        for dy in (1, 3, 2):
            l2(dy).wait_recv()
            l4((y + 4 - dy) % 4, k).start()

    def left_product():
        for yy in range(4):
            l4(yy, 1 - k).wait_recv()

        def part(c, carry):
            b = lbuf[pl.ds(c * 8, 8)].reshape(384, LC)
            return carry + jnp.dot(lrows[c], b, preferred_element_type=F32)

        lpr[...] = lax.fori_loop(0, 8, part, jnp.zeros((192, LC), F32))
        v = lpr[...]
        lsq[row] = jnp.broadcast_to(jnp.sum(v * v, axis=0, keepdims=True), (8, LC))
        each(16, l3, "start")
        pltpu.make_async_copy(lpr, lprod_o, cp.at[6]).start()

    def make_product(t):
        lo, n = TILES[t]
        pltpu.make_async_copy(acc.at[pl.ds(lo, n)], rnew_o.at[pl.ds(lo, n)], cp.at[8 + t]).start()

        m = PIECE[t]

        def first(cc, carry):
            half = acc[pl.ds(lo, n // 2), :].astype(BF16)
            for e in range(4):
                c = ((x + e) % 4) * 2 + cc
                d = jnp.dot(half, bas[c].reshape(SC, 256), preferred_element_type=F32)
                for i in (0, 1):
                    for s in (0, 1):
                        v = d[i * m : (i + 1) * m, s * 128 : (s + 1) * 128]
                        if e == 2:
                            away[i, 0, cc * 2 + s, spot(t), :] = v.astype(BF16)
                        elif e == (3 if i == 0 else 1):
                            away[i, 1, cc * 2 + s, spot(t), :] = v.astype(BF16)
                        else:
                            near[i, 0 if e == 0 else 1, cc * 2 + s, spot(t), :] = v
            return carry

        lax.fori_loop(0, 2, first, 0)

        def second(c, carry):
            half = acc[pl.ds(lo + n // 2, n // 2), :].astype(BF16)
            d = jnp.dot(half, bas[c].reshape(SC, 256), preferred_element_type=F32)
            for i in (0, 1):
                for s in (0, 1):
                    v = d[i * m : (i + 1) * m, s * 128 : (s + 1) * 128]
                    both[i, (c % 2) * 2 + s, c // 2, spot(t), :] = v.astype(BF16)
                    whole[i, (c % 2) * 2 + s, c // 2, spot(t), :] = v
            return carry

        lax.fori_loop(0, 8, second, 0)

    TYPES = (0, 1, 2, 3)

    def hd(i):
        return i // 2, 1 if i % 2 == 0 else -1

    def rows_of(i, t):
        return pl.ds(TILES[t][0] + i * PIECE[t], PIECE[t])

    def spot(t):
        return pl.ds(PLACE[t], PIECE[t])

    def pos(h, axis):
        return x if (h == 0) == (axis == FIRST) else z

    def parcel(i, t, kind):
        h, d = hd(i)
        if h == 0:
            return away.at[i, 0 if kind == A1 else 1, :, spot(t), :]
        return both.at[i - 2, (z + (2 if kind == A1 else -d) + 4) % 4, :, spot(t), :]

    def kept(i, t, ahead):
        h, d = hd(i)
        if h == 0:
            return near.at[i, 1 if ahead else 0, :, spot(t), :]
        return whole.at[i - 2, (z + (d if ahead else 0) + 4) % 4, :, spot(t), :]

    def rs(kind, i, t):
        h, d = hd(i)
        axis = FIRST if kind < A2 else SECOND
        q = (pos(h, SECOND) + 4) % 4
        if kind == A1:
            src, dst, to = parcel(i, t, A1), ra.at[i, :, spot(t), :], d
        elif kind == B1:
            src, dst, to = tb.at[i, :, spot(t), :], rb.at[i, :, spot(t), :], d
        elif kind == C1:
            src, dst, to = parcel(i, t, C1), rc.at[i, :, spot(t), :], -d
        elif kind == A2:
            src, dst, to = s1.at[i, (q + 2) % 4, spot(t), :], ra2.at[i, spot(t), :], d
        elif kind == B2:
            src, dst, to = tb2.at[i, spot(t), :], rb2.at[i, spot(t), :], d
        else:
            src, dst, to = s1.at[i, (q - d + 4) % 4, spot(t), :], rc2.at[i, spot(t), :], -d
        return pltpu.make_async_remote_copy(
            src_ref=src, dst_ref=dst, send_sem=rs_s.at[kind, i * 4 + t], recv_sem=rs_r.at[kind, i * 4 + t],
            device_id=neighbour(h, axis, to), device_id_type=MESH,
        )

    def r0(t):
        for kind in (A1, C1):
            for i in TYPES:
                rs(kind, i, t).start()

    def r1(t):
        for i in TYPES:
            h, d = hd(i)
            rs(A1, i, t).wait_recv()
            tb[i, :, spot(t), :] = (kept(i, t, True)[...] + ra[i, :, spot(t), :].astype(F32)).astype(BF16)
            rs(B1, i, t).start()

    def r2(t):
        for i in TYPES:
            h, d = hd(i)
            rs(C1, i, t).wait_recv()
            rs(B1, i, t).wait_recv()
            total = kept(i, t, False)[...] + rb[i, :, spot(t), :].astype(F32) + rc[i, :, spot(t), :].astype(F32)
            s1[i, :, spot(t), :] = total.astype(BF16)
            rs(A2, i, t).start()
            rs(C2, i, t).start()
            q = pos(h, SECOND)
            for f, e in ((0, 0), (1, d)):
                w = (q + e + 4) % 4
                mine = kept(i, t, False).at[w]
                keep[f, i, spot(t), :] = (
                    mine[...] + rb[i, w, spot(t), :].astype(F32) + rc[i, w, spot(t), :].astype(F32)
                )

    def r3(t):
        for i in TYPES:
            h, d = hd(i)
            rs(A2, i, t).wait_recv()
            tb2[i, spot(t), :] = (keep[1, i, spot(t), :] + ra2[i, spot(t), :].astype(F32)).astype(BF16)
            rs(B2, i, t).start()

    def r4(t):
        total = jnp.zeros((8, 128), F32)
        for i in TYPES:
            rs(C2, i, t).wait_recv()
            rs(B2, i, t).wait_recv()
            v = keep[0, i, spot(t), :] + rb2[i, spot(t), :].astype(F32) + rc2[i, spot(t), :].astype(F32)
            rout[rows_of(i, t), :] = v
            total = total + jnp.sum((v * v).reshape(PIECE[t] // 8, 8, 128), axis=0)
        lo, n = TILES[t]
        pltpu.make_async_copy(rout.at[pl.ds(lo, n)], rprod_o.at[pl.ds(lo, n)], cp.at[12 + t]).start()
        return total

    H = (0, 1)
    b_sends, b_sibs = [], []

    def begin(send, sibs):
        for c in send + sibs:
            c.start()
        b_sends.extend(send)
        b_sibs.extend(sibs)

    for u in range(16):
        arrive(G, u)
        onward(G, u)
        source_unit(u)
        for hops in (1, 2, 3):
            relay_to(hops, u + 1 - LAGS[hops - 1])
        if u == 2:
            begin([b_send(0, 0, "full", 1), b_send(1, 0, "full", -1)], [b_sib(0, 0, k)])
        if u == 8:
            b_send(0, -1, "full", 1).wait_recv()
            b_send(1, 1, "full", -1).wait_recv()
            begin([b_send(2, -1, 0, 1), b_send(3, 1, 1, -1)], [b_sib(1, -1, k), b_sib(2, 1, k)])
        if u == 12:
            onward(L, 0)
    relay_to(1, 16)
    relay_to(2, 16)
    b_send(2, 2, 0, 1).wait_recv()
    b_send(3, 2, 1, -1).wait_recv()
    begin([], [b_sib(3, 2, k)])

    def lb(a, b):
        for u in range(a, b):
            arrive(L, u)
            onward(L, u)

    lb(1, 3)
    late[0].wait()
    relay_to(3, 11)
    group_ready(0)
    gram(0, True, 0, 7)
    lb(3, 6)
    relay_to(3, 14)
    group_ready(-1)
    gram(-1, False, 0, 7)
    lb(6, 10)
    relay_to(3, 15)
    group_ready(1)
    gram(1, False, 0, 7)
    lb(10, 13)
    relay_to(3, 16)
    for i, dy in enumerate((0, -1, 1, 2)):
        b_sib(i, dy, 1 - k).wait_recv()
    group_ready(2)
    gram(2, False, 0, 2)
    make_product(0)
    r0(0)
    gram(2, False, 2, 4)
    make_product(1)
    r0(1)
    for dx in (0, -1, 1, 2):
        left(dx)
    r1(0)
    gram(2, False, 4, 6)
    make_product(2)
    r0(2)
    left_join()
    r1(1)
    gram(2, False, 6, 7)
    make_product(3)
    r0(3)
    r1(2)
    lb(13, 16)
    r2(0)
    late[1].wait()
    left_refresh()
    r1(3)
    r3(0)
    r2(1)
    total = r4(0)
    left_share()
    r3(1)
    r2(2)
    total = total + r4(1)
    left_product()
    r3(2)
    r2(3)
    total = total + r4(2)
    r3(3)
    total = total + r4(3)
    rsq[col] = total
    each(8, rq, "start")

    each(16, l3, "wait_recv")
    lsum = pltpu.make_async_copy(lsq, lsum_o, cp.at[7])
    lsum.start()
    each(8, rq, "wait_recv")
    rsum = pltpu.make_async_copy(rsq, rsum_o, cp.at[16])
    rsum.start()

    for c in sent + b_sends + b_sibs:
        c.wait_send()
    for df, ds in UNITS:
        for h in H:
            ref = unit_region(h, df, ds)

            @pl.when(jnp.logical_and(is_k, hop(h) != 3))
            def _():
                to_y(ref, h, df, ds).wait_send()

            @pl.when(is_k)
            def _():
                to_sib(ref, h, df, ds).wait_send()

    for kind in range(6):
        for i in TYPES:
            for t in range(4):
                rs(kind, i, t).wait_send()
    for yy in range(4):
        l0(yy, yy * 2 + 1 - k).wait_send()
        l4(yy, k).wait_send()
    for dy in (1, 2, 3):
        l1(dy).wait_send()
        l2(dy).wait_send()
    each(16, l3, "wait_send")
    each(8, rq, "wait_send")
    for t, (lo, n) in enumerate(TILES):
        pltpu.make_async_copy(acc.at[pl.ds(lo, n)], rnew_o.at[pl.ds(lo, n)], cp.at[8 + t]).wait()
        pltpu.make_async_copy(rout.at[pl.ds(lo, n)], rprod_o.at[pl.ds(lo, n)], cp.at[12 + t]).wait()
    pltpu.make_async_copy(ln, lnew_o, cp.at[5]).wait()
    pltpu.make_async_copy(lpr, lprod_o, cp.at[6]).wait()
    lsum.wait()
    rsum.wait()


def refresh(gradient, left_basis, right_basis, right_factor, left_factor):
    dma = pltpu.SemaphoreType.DMA
    n = len(AG)
    any_spec = pl.BlockSpec(memory_space=pl.ANY)
    V = pltpu.VMEM
    return pl.pallas_call(
        kernel,
        out_shape=(
            jax.ShapeDtypeStruct((GC, SC), F32),
            jax.ShapeDtypeStruct((GC, 128), F32),
            jax.ShapeDtypeStruct((8, 8, 128), F32),
            jax.ShapeDtypeStruct((192, LC), F32),
            jax.ShapeDtypeStruct((192, LC), F32),
            jax.ShapeDtypeStruct((16, 8, LC), F32),
        ),
        in_specs=[any_spec] * 5,
        out_specs=[any_spec] * 6,
        scratch_shapes=[
            V((64, 48, GC), BF16), V((64, 48, LC), BF16), V((64, 48, SC), BF16), V((GC, SC), F32),
            V((8, 2, 448, 256), BF16), V((8, 192, LC), BF16),
            V((2, 2, 4, 448, 128), BF16), V((2, 2, 4, 448, 128), F32),
            V((2, 4, 4, 448, 128), BF16), V((2, 4, 4, 448, 128), F32),
            V((4, 4, 448, 128), BF16), V((4, 4, 448, 128), BF16), V((4, 4, 448, 128), BF16),
            V((4, 4, 448, 128), BF16), V((4, 4, 448, 128), BF16), V((2, 4, 448, 128), F32),
            V((4, 448, 128), BF16), V((4, 448, 128), BF16), V((4, 448, 128), BF16), V((4, 448, 128), BF16),
            V((GC, 128), F32), V((8, 8, 128), F32),
            V((4, 192, LC), BF16), V((4, 192, LC), BF16), V((4, 192, LC), BF16), V((8, 192, LC), BF16),
            V((192, LC), F32), V((192, LC), F32), V((192, LC), F32), V((16, 8, LC), F32),
            dma((n,)), dma((n,)), dma((n,)), dma((n,)),
            dma((32,)), dma((32,)), dma((32,)), dma((32,)), dma((32,)),
            dma((4,)), dma((4,)), dma((4,)), dma((4,)), dma((17,)),
            dma((6, 16)), dma((6, 16)),
            dma((4,)), dma((4,)), dma((4,)), dma((4,)), dma((4,)), dma((4,)), dma((4,)), dma((4,)),
            dma((16,)), dma((16,)), dma((8,)), dma((8,)),
        ],
        compiler_params=pltpu.CompilerParams(
            collective_id=0, has_side_effects=True, vmem_limit_bytes=67043328
        ),
        name="refresh",
    )(
        gradient.reshape(4, 48, GC), left_basis.reshape(4, 48, LC), right_basis.reshape(2, 448, 256),
        right_factor, left_factor,
    )


def on_device(gradient, left_factor, right_factor, left_basis, right_basis):
    right_new, right_prod, rsq, left_new, left_prod, lsq = refresh(
        gradient, left_basis, right_basis, right_factor, left_factor
    )
    left_sq = jnp.sum(lsq[:, 0], axis=0)
    right_sq = jnp.sum(rsq, axis=(0, 1))
    left_out = left_prod * lax.rsqrt(left_sq / DMODEL + epsilon)
    right_out = right_prod * lax.rsqrt(right_sq / DHIDDEN + epsilon)
    return (left_new, right_new, left_out, right_out)


def solution(mesh):
    in_specs = (P("row", "col"), P("row", "col"), P("col", "row"), P("row", "col"), P("row", "col"))
    out_specs = (P("row", "col"), P("col", "row"), P("row", "col"), P("col", "row"))
    return jax.shard_map(on_device, mesh=mesh, in_specs=in_specs, out_specs=out_specs, check_vma=False)
```

time: 192 us -> 170 us (0.89)
  Pallas kernels: 178 us -> 156 us
    pallas_call x1, Pallas kernels: 178 us -> 156 us  [refresh(): pl.pallas_call(kernel, out_shape=(jax.ShapeDtypeStruct((GC, SC), F32), ja...]
where the time goes in v3:
time: 170 us
  Pallas kernels  156 us (92%)
  local copies, waits for them, and re-layouts  7.67 us (5%)
  other arithmetic  5.62 us (3%)
    pallas_call x1, Pallas kernels, refresh(): pl.pallas_call(kernel, out_shape=(jax.ShapeDtypeStruct((GC, SC), F32), ja...  156 us
    unnamed x2, local copies, waits for them, and re-layouts  7.67 us

profile of v3, /device:TPU:1, one launch (start us, length us, event | category | flops | bytes accessed | tf_op | source)
XLA Modules:
  0.0 170.1 jit_solution(1645255909289264664)
XLA Ops:
  0.6 156.2 %refresh.1 = (f32[1792,896]{1,0:T(8,128)}, f32[1792,128]{1,0:T(8,128)}, f32[8,8,128]{2,1,0:T(8,128)}, f32[192,384]{1,0:T(8,128)}, f32[192,384]{1,0:T(8,128)}, /*index=5*/f32[16,8,384]{2,1,0:T(8,128)}) custom-call(bf16[4,48,1792]{2,1,0:T(8,128)(2,1)} %bitcast.3, bf16[4,48,384]{2,1,0:T(8,128)(2,1)} %bitcast.5, bf16[2,448,256]{2,1,0:T(8,128)(2,1)} %bitcast.4, ...), custom_call_target="tpu_custom_call" | custom-call | tf_op jit(solution)/shard_map/refresh/pallas_call | solution.py:663
  156.8 0.8 reduce_sum.19
  157.6 2.2 %broadcast_multiply_fusion = f32[1792,128]{1,0:T(8,128)} fusion(f32[1792,128]{1,0:T(8,128)} %get-tuple-element.14, f32[128]{0:T(128)S(1)} %add_rsqrt_fusion.1), kind=kLoop, calls=%fused_computation | loop fusion | flops 229376 | bytes 1835520 | tf_op jit(solution)/shard_map/mul | solution.py:710
  159.8 1.0 slice_reduce_fusion
  160.7 1.7 broadcast_multiply_fusion.1
  162.4 1.7 copy.11
  164.1 6.0 %copy.12 = f32[1792,896]{1,0:T(8,128)} copy(f32[1792,896]{1,0:T(8,128)} %get-tuple-element.21) | data formatting | bytes 12845056
  (2 shorter events, 0.0 us)

commit v4 on v3

--- a/solution.py
+++ b/solution.py
@@ -20,7 +20,7 @@
 FIRST, SECOND = "f", "s"
 TILES = ((0, 512), (512, 512), (1024, 512), (1536, 256))
 PIECE = [n // 4 for _, n in TILES]
-PLACE = [0, 128, 256, 384]
+PLACE = [sum(PIECE[:t]) for t in range(len(TILES))]
 A1, B1, C1, A2, B2, C2 = range(6)
 
 
@@ -274,18 +274,16 @@
         xg = (x + dx + 4) % 4
         rows = pl.ds(xg * 16, 16)
 
-        def tile(m, carry):
-            cols = pl.ds(pl.multiple_of(m * 256, 256), 256)
-            a = slab[rows, :, cols].reshape(768, 256)
+        for t in range(lo, hi):
+            start, n = TILES[t]
+            cols = pl.ds(start, n)
+            a = slab[rows, :, cols].reshape(768, n)
             b = shared[rows].reshape(768, SC)
             d = lax.dot_general(a, b, (((0,), (0,)), ((), ())), preferred_element_type=F32)
             old = acc[cols, :]
             if first:
                 old = ema_decay * old
             acc[cols, :] = old + (1.0 - ema_decay) * d
-            return carry
-
-        lax.fori_loop(lo, hi, tile, 0)
 
     def l0(yy, c):
         return pltpu.make_async_remote_copy(
@@ -397,15 +395,18 @@
 
         m = PIECE[t]
 
-        def first(cc, carry):
-            half = acc[pl.ds(lo, n // 2), :].astype(BF16)
+        def block(cc, carry):
+            half = acc[pl.ds(lo, n), :].astype(BF16)
             for e in range(4):
-                c = ((x + e) % 4) * 2 + cc
-                d = jnp.dot(half, bas[c].reshape(SC, 256), preferred_element_type=F32)
-                for i in (0, 1):
+                xo = (x + e) % 4
+                d = jnp.dot(half, bas[xo * 2 + cc].reshape(SC, 256), preferred_element_type=F32)
+                for i in range(4):
                     for s in (0, 1):
                         v = d[i * m : (i + 1) * m, s * 128 : (s + 1) * 128]
-                        if e == 2:
+                        if i >= 2:
+                            both[i - 2, cc * 2 + s, xo, spot(t), :] = v.astype(BF16)
+                            whole[i - 2, cc * 2 + s, xo, spot(t), :] = v
+                        elif e == 2:
                             away[i, 0, cc * 2 + s, spot(t), :] = v.astype(BF16)
                         elif e == (3 if i == 0 else 1):
                             away[i, 1, cc * 2 + s, spot(t), :] = v.astype(BF16)
@@ -413,19 +414,7 @@
                             near[i, 0 if e == 0 else 1, cc * 2 + s, spot(t), :] = v
             return carry
 
-        lax.fori_loop(0, 2, first, 0)
-
-        def second(c, carry):
-            half = acc[pl.ds(lo + n // 2, n // 2), :].astype(BF16)
-            d = jnp.dot(half, bas[c].reshape(SC, 256), preferred_element_type=F32)
-            for i in (0, 1):
-                for s in (0, 1):
-                    v = d[i * m : (i + 1) * m, s * 128 : (s + 1) * 128]
-                    both[i, (c % 2) * 2 + s, c // 2, spot(t), :] = v.astype(BF16)
-                    whole[i, (c % 2) * 2 + s, c // 2, spot(t), :] = v
-            return carry
-
-        lax.fori_loop(0, 8, second, 0)
+        lax.fori_loop(0, 2, block, 0)
 
     TYPES = (0, 1, 2, 3)
 
@@ -531,6 +520,11 @@
         b_sends.extend(send)
         b_sibs.extend(sibs)
 
+    def lb(a, b):
+        for u in range(a, b):
+            arrive(L, u)
+            onward(L, u)
+
     for u in range(16):
         arrive(G, u)
         onward(G, u)
@@ -545,50 +539,47 @@
             begin([b_send(2, -1, 0, 1), b_send(3, 1, 1, -1)], [b_sib(1, -1, k), b_sib(2, 1, k)])
         if u == 12:
             onward(L, 0)
+        if u == 15:
+            lb(1, 3)
+        if u == 14:
+            late[0].wait()
+            relay_to(3, 11)
+            group_ready(0)
+            gram(0, True, 0, 4)
     relay_to(1, 16)
+    lb(3, 6)
     relay_to(2, 16)
     b_send(2, 2, 0, 1).wait_recv()
     b_send(3, 2, 1, -1).wait_recv()
     begin([], [b_sib(3, 2, k)])
 
-    def lb(a, b):
-        for u in range(a, b):
-            arrive(L, u)
-            onward(L, u)
-
-    lb(1, 3)
-    late[0].wait()
-    relay_to(3, 11)
-    group_ready(0)
-    gram(0, True, 0, 7)
-    lb(3, 6)
     relay_to(3, 14)
     group_ready(-1)
-    gram(-1, False, 0, 7)
+    gram(-1, False, 0, 4)
     lb(6, 10)
     relay_to(3, 15)
     group_ready(1)
-    gram(1, False, 0, 7)
-    lb(10, 13)
+    gram(1, False, 0, 4)
     relay_to(3, 16)
     for i, dy in enumerate((0, -1, 1, 2)):
         b_sib(i, dy, 1 - k).wait_recv()
     group_ready(2)
-    gram(2, False, 0, 2)
+    gram(2, False, 0, 1)
     make_product(0)
     r0(0)
-    gram(2, False, 2, 4)
+    lb(10, 13)
+    gram(2, False, 1, 2)
     make_product(1)
     r0(1)
     for dx in (0, -1, 1, 2):
         left(dx)
     r1(0)
-    gram(2, False, 4, 6)
+    gram(2, False, 2, 3)
     make_product(2)
     r0(2)
     left_join()
     r1(1)
-    gram(2, False, 6, 7)
+    gram(2, False, 3, 4)
     make_product(3)
     r0(3)
     r1(2)
@@ -700,15 +691,43 @@
     )
 
 
+def finish_kernel(rnew, rprod, rsq, lnew, lprod, lsq, lnew_o, rnew_o, lout_o, rout_o):
+    rnew_o[...] = rnew[...]
+    right_sq = jnp.sum(rsq[...].reshape(64, 128), axis=0, keepdims=True)
+    rout_o[...] = rprod[...] * lax.rsqrt(right_sq / DHIDDEN + epsilon)
+
+    @pl.when(pl.program_id(0) == 0)
+    def _():
+        lnew_o[...] = lnew[...]
+        left_sq = jnp.sum(lsq[...], axis=0)[:1]
+        lout_o[...] = lprod[...] * lax.rsqrt(left_sq / DMODEL + epsilon)
+
+
+def finish(right_new, right_prod, rsq, left_new, left_prod, lsq):
+    def rows(n):
+        return pl.BlockSpec((448, n), lambda i: (i, 0))
+
+    def whole(*shape):
+        return pl.BlockSpec(shape, lambda i: (0,) * len(shape))
+
+    return pl.pallas_call(
+        finish_kernel,
+        grid=(4,),
+        out_shape=(
+            jax.ShapeDtypeStruct((192, LC), F32),
+            jax.ShapeDtypeStruct((GC, SC), F32),
+            jax.ShapeDtypeStruct((192, LC), F32),
+            jax.ShapeDtypeStruct((GC, 128), F32),
+        ),
+        in_specs=[rows(SC), rows(128), whole(8, 8, 128), whole(192, LC), whole(192, LC), whole(16, 8, LC)],
+        out_specs=(whole(192, LC), rows(SC), whole(192, LC), rows(128)),
+        compiler_params=pltpu.CompilerParams(vmem_limit_bytes=60 * 1024 * 1024),
+        name="finish",
+    )(right_new, right_prod, rsq, left_new, left_prod, lsq)
+
+
 def on_device(gradient, left_factor, right_factor, left_basis, right_basis):
-    right_new, right_prod, rsq, left_new, left_prod, lsq = refresh(
-        gradient, left_basis, right_basis, right_factor, left_factor
-    )
-    left_sq = jnp.sum(lsq[:, 0], axis=0)
-    right_sq = jnp.sum(rsq, axis=(0, 1))
-    left_out = left_prod * lax.rsqrt(left_sq / DMODEL + epsilon)
-    right_out = right_prod * lax.rsqrt(right_sq / DHIDDEN + epsilon)
-    return (left_new, right_new, left_out, right_out)
+    return finish(*refresh(gradient, left_basis, right_basis, right_factor, left_factor))
 
 
 def solution(mesh):

time: 170 us -> 155 us (0.912)
  local copies, waits for them, and re-layouts: 7.67 us -> 0 us
  other arithmetic: 5.62 us -> 0 us
  Pallas kernels: 156 us -> 154 us
    pallas_call x1, Pallas kernels: 156 us -> 147 us  [refresh(): pl.pallas_call(kernel, out_shape=(jax.ShapeDtypeStruct((GC, SC), F32), ja...]
    unnamed x2 -> x0, local copies, waits for them, and re-layouts: 7.67 us -> none
    pallas_call x0 -> x1, Pallas kernels: none -> 6.92 us  [finish(): pl.pallas_call(finish_kernel, grid=(4,), out_shape=(jax.ShapeDtypeStruct(...]
    mul x2 -> x0, other arithmetic: 3.86 us -> none  [the longest x1 2.17 us: on_device(): right_out = right_prod * lax.rsqrt(right_sq / DHIDDEN + epsilon)]
    reduce_sum x2 -> x0, other arithmetic: 1.74 us -> none  [the longest x1 0.96 us: on_device(): left_sq = jnp.sum(lsq[:, 0], axis=0)]
where the time goes in v4:
time: 155 us
  Pallas kernels  154 us (99%)
    pallas_call x1, Pallas kernels, refresh(): pl.pallas_call(kernel, out_shape=(jax.ShapeDtypeStruct((GC, SC), F32), ja...  147 us
    pallas_call x1, Pallas kernels, finish(): pl.pallas_call(finish_kernel, grid=(4,), out_shape=(jax.ShapeDtypeStruct(...  6.92 us

profile of v4, /device:TPU:1, one launch (start us, length us, event | category | flops | bytes accessed | tf_op | source)
XLA Modules:
  0.0 155.1 jit_solution(10536831465958706656)
XLA Ops:
  0.6 147.5 %refresh.1 = (f32[1792,896]{1,0:T(8,128)}, f32[1792,128]{1,0:T(8,128)}, f32[8,8,128]{2,1,0:T(8,128)}, f32[192,384]{1,0:T(8,128)}, f32[192,384]{1,0:T(8,128)}, /*index=5*/f32[16,8,384]{2,1,0:T(8,128)}) custom-call(bf16[4,48,1792]{2,1,0:T(8,128)(2,1)} %bitcast.3, bf16[4,48,384]{2,1,0:T(8,128)(2,1)} %bitcast.5, bf16[2,448,256]{2,1,0:T(8,128)(2,1)} %bitcast.4, ...), custom_call_target="tpu_custom_call" | custom-call | tf_op jit(solution)/shard_map/refresh/pallas_call | solution.py:654
  148.1 6.9 %finish.1 = (f32[192,384]{1,0:T(8,128)}, f32[1792,896]{1,0:T(8,128)}, f32[192,384]{1,0:T(8,128)}, f32[1792,128]{1,0:T(8,128)}) custom-call(f32[1792,896]{1,0:T(8,128)} %get-tuple-element.10.rnew, f32[1792,128]{1,0:T(8,128)} %get-tuple-element.11.rprod, f32[8,8,128]{2,1,0:T(8,128)} %get-tuple-element.12.rsq, f32[192,384]{1,0:T(8,128)} %get-tuple-element.13.lnew, ...), custom_call_target="tpu_custom_call" | custom-call | tf_op jit(solution)/shard_map/finish/pallas_call | solution.py:713

commit v5 on v4

--- a/solution.py
+++ b/solution.py
@@ -55,10 +55,10 @@
 
 def kernel(
     grad, lbas, rbas, rfac, lfac,
-    rnew_o, rprod_o, rsum_o, lnew_o, lprod_o, lsum_o,
-    slab, lbuf, shared, acc, bas, lp, away, near, both, whole,
-    ra, tb, rb, rc, s1, keep, ra2, tb2, rb2, rc2, rout, rsq,
-    lsib, lmid, lrecv, lrows, lf, ln, lpr, lsq,
+    acc, rout, rsum, ln, lpr, lsum,
+    slab, lbuf, shared, bas, lp, away, near, both, whole,
+    ra, tb, rb, rc, s1, keep, ra2, tb2, rb2, rc2, rsq,
+    lsib, lmid, lrecv, lrows, lf, lsq,
     ag_s, ag_r, lg_s, lg_r, y_s, y_r, sib_s, sib_r, loc, bs, br, bss, bsr, cp,
     rs_s, rs_r, l0s, l0r, l1s, l1r, l2s, l2r, l4s, l4r, l3s, l3r, q_s, q_r,
 ):
@@ -368,7 +368,6 @@
         for dy in (1, 3, 2):
             l2(dy).start()
         l4(y, k).start()
-        pltpu.make_async_copy(ln, lnew_o, cp.at[5]).start()
 
     def left_share():
         for dy in (1, 3, 2):
@@ -387,11 +386,9 @@
         v = lpr[...]
         lsq[row] = jnp.broadcast_to(jnp.sum(v * v, axis=0, keepdims=True), (8, LC))
         each(16, l3, "start")
-        pltpu.make_async_copy(lpr, lprod_o, cp.at[6]).start()
 
     def make_product(t):
         lo, n = TILES[t]
-        pltpu.make_async_copy(acc.at[pl.ds(lo, n)], rnew_o.at[pl.ds(lo, n)], cp.at[8 + t]).start()
 
         m = PIECE[t]
 
@@ -507,8 +504,6 @@
             v = keep[0, i, spot(t), :] + rb2[i, spot(t), :].astype(F32) + rc2[i, spot(t), :].astype(F32)
             rout[rows_of(i, t), :] = v
             total = total + jnp.sum((v * v).reshape(PIECE[t] // 8, 8, 128), axis=0)
-        lo, n = TILES[t]
-        pltpu.make_async_copy(rout.at[pl.ds(lo, n)], rprod_o.at[pl.ds(lo, n)], cp.at[12 + t]).start()
         return total
 
     H = (0, 1)
@@ -605,11 +600,9 @@
     each(8, rq, "start")
 
     each(16, l3, "wait_recv")
-    lsum = pltpu.make_async_copy(lsq, lsum_o, cp.at[7])
-    lsum.start()
+    lsum[...] = jnp.sum(lsq[...], axis=0)
     each(8, rq, "wait_recv")
-    rsum = pltpu.make_async_copy(rsq, rsum_o, cp.at[16])
-    rsum.start()
+    rsum[...] = jnp.sum(rsq[...], axis=0)
 
     for c in sent + b_sends + b_sibs:
         c.wait_send()
@@ -637,13 +630,6 @@
         l2(dy).wait_send()
     each(16, l3, "wait_send")
     each(8, rq, "wait_send")
-    for t, (lo, n) in enumerate(TILES):
-        pltpu.make_async_copy(acc.at[pl.ds(lo, n)], rnew_o.at[pl.ds(lo, n)], cp.at[8 + t]).wait()
-        pltpu.make_async_copy(rout.at[pl.ds(lo, n)], rprod_o.at[pl.ds(lo, n)], cp.at[12 + t]).wait()
-    pltpu.make_async_copy(ln, lnew_o, cp.at[5]).wait()
-    pltpu.make_async_copy(lpr, lprod_o, cp.at[6]).wait()
-    lsum.wait()
-    rsum.wait()
 
 
 def refresh(gradient, left_basis, right_basis, right_factor, left_factor):
@@ -654,35 +640,35 @@
     return pl.pallas_call(
         kernel,
         out_shape=(
-            jax.ShapeDtypeStruct((GC, SC), F32),
-            jax.ShapeDtypeStruct((GC, 128), F32),
-            jax.ShapeDtypeStruct((8, 8, 128), F32),
-            jax.ShapeDtypeStruct((192, LC), F32),
-            jax.ShapeDtypeStruct((192, LC), F32),
-            jax.ShapeDtypeStruct((16, 8, LC), F32),
+            V((GC, SC), F32),
+            V((GC, 128), F32),
+            V((8, 128), F32),
+            V((192, LC), F32),
+            V((192, LC), F32),
+            V((8, LC), F32),
         ),
         in_specs=[any_spec] * 5,
-        out_specs=[any_spec] * 6,
+        out_specs=[pl.BlockSpec(memory_space=pltpu.VMEM)] * 6,
         scratch_shapes=[
-            V((64, 48, GC), BF16), V((64, 48, LC), BF16), V((64, 48, SC), BF16), V((GC, SC), F32),
+            V((64, 48, GC), BF16), V((64, 48, LC), BF16), V((64, 48, SC), BF16),
             V((8, 2, 448, 256), BF16), V((8, 192, LC), BF16),
             V((2, 2, 4, 448, 128), BF16), V((2, 2, 4, 448, 128), F32),
             V((2, 4, 4, 448, 128), BF16), V((2, 4, 4, 448, 128), F32),
             V((4, 4, 448, 128), BF16), V((4, 4, 448, 128), BF16), V((4, 4, 448, 128), BF16),
             V((4, 4, 448, 128), BF16), V((4, 4, 448, 128), BF16), V((2, 4, 448, 128), F32),
             V((4, 448, 128), BF16), V((4, 448, 128), BF16), V((4, 448, 128), BF16), V((4, 448, 128), BF16),
-            V((GC, 128), F32), V((8, 8, 128), F32),
+            V((8, 8, 128), F32),
             V((4, 192, LC), BF16), V((4, 192, LC), BF16), V((4, 192, LC), BF16), V((8, 192, LC), BF16),
-            V((192, LC), F32), V((192, LC), F32), V((192, LC), F32), V((16, 8, LC), F32),
+            V((192, LC), F32), V((16, 8, LC), F32),
             dma((n,)), dma((n,)), dma((n,)), dma((n,)),
             dma((32,)), dma((32,)), dma((32,)), dma((32,)), dma((32,)),
-            dma((4,)), dma((4,)), dma((4,)), dma((4,)), dma((17,)),
+            dma((4,)), dma((4,)), dma((4,)), dma((4,)), dma((5,)),
             dma((6, 16)), dma((6, 16)),
             dma((4,)), dma((4,)), dma((4,)), dma((4,)), dma((4,)), dma((4,)), dma((4,)), dma((4,)),
             dma((16,)), dma((16,)), dma((8,)), dma((8,)),
         ],
         compiler_params=pltpu.CompilerParams(
-            collective_id=0, has_side_effects=True, vmem_limit_bytes=67043328
+            collective_id=0, has_side_effects=True, vmem_limit_bytes=58800000
         ),
         name="refresh",
     )(
@@ -691,39 +677,39 @@
     )
 
 
-def finish_kernel(rnew, rprod, rsq, lnew, lprod, lsq, lnew_o, rnew_o, lout_o, rout_o):
-    rnew_o[...] = rnew[...]
-    right_sq = jnp.sum(rsq[...].reshape(64, 128), axis=0, keepdims=True)
-    rout_o[...] = rprod[...] * lax.rsqrt(right_sq / DHIDDEN + epsilon)
-
-    @pl.when(pl.program_id(0) == 0)
-    def _():
-        lnew_o[...] = lnew[...]
-        left_sq = jnp.sum(lsq[...], axis=0)[:1]
-        lout_o[...] = lprod[...] * lax.rsqrt(left_sq / DMODEL + epsilon)
-
-
-def finish(right_new, right_prod, rsq, left_new, left_prod, lsq):
-    def rows(n):
-        return pl.BlockSpec((448, n), lambda i: (i, 0))
-
-    def whole(*shape):
-        return pl.BlockSpec(shape, lambda i: (0,) * len(shape))
-
+def finish_kernel(rnew, rprod, rsum, lnew, lprod, lsum, lnew_o, rnew_o, lout_o, rout_o, rout, lout, sem):
+    copies = [pltpu.make_async_copy(rnew, rnew_o, sem.at[0]), pltpu.make_async_copy(lnew, lnew_o, sem.at[1])]
+    for c in copies:
+        c.start()
+    right_sq = jnp.sum(rsum[...], axis=0, keepdims=True)
+    rout[...] = rprod[...] * lax.rsqrt(right_sq / DHIDDEN + epsilon)
+    copies.append(pltpu.make_async_copy(rout, rout_o, sem.at[2]))
+    copies[2].start()
+    lout[...] = lprod[...] * lax.rsqrt(lsum[:1, :] / DMODEL + epsilon)
+    copies.append(pltpu.make_async_copy(lout, lout_o, sem.at[3]))
+    copies[3].start()
+    for c in copies:
+        c.wait()
+
+
+def finish(*results):
+    vmem = pl.BlockSpec(memory_space=pltpu.VMEM)
     return pl.pallas_call(
         finish_kernel,
-        grid=(4,),
         out_shape=(
             jax.ShapeDtypeStruct((192, LC), F32),
             jax.ShapeDtypeStruct((GC, SC), F32),
             jax.ShapeDtypeStruct((192, LC), F32),
             jax.ShapeDtypeStruct((GC, 128), F32),
         ),
-        in_specs=[rows(SC), rows(128), whole(8, 8, 128), whole(192, LC), whole(192, LC), whole(16, 8, LC)],
-        out_specs=(whole(192, LC), rows(SC), whole(192, LC), rows(128)),
-        compiler_params=pltpu.CompilerParams(vmem_limit_bytes=60 * 1024 * 1024),
+        in_specs=[vmem] * 6,
+        out_specs=[pl.BlockSpec(memory_space=pl.ANY)] * 4,
+        scratch_shapes=[
+            pltpu.VMEM((GC, 128), F32), pltpu.VMEM((192, LC), F32), pltpu.SemaphoreType.DMA((4,)),
+        ],
+        compiler_params=pltpu.CompilerParams(vmem_limit_bytes=24 * 1024 * 1024),
         name="finish",
-    )(right_new, right_prod, rsq, left_new, left_prod, lsq)
+    )(*[pltpu.with_memory_space_constraint(r, pltpu.VMEM) for r in results])
 
 
 def on_device(gradient, left_factor, right_factor, left_basis, right_basis):

time: 155 us -> 151 us (0.974)
  Pallas kernels: 154 us -> 150 us
    pallas_call x2, Pallas kernels: 154 us -> 150 us  [the longest x1 147 us: refresh(): pl.pallas_call(kernel, out_shape=(V((GC, SC), F32), V((GC, 128), F32), V(...]
where the time goes in v5:
time: 151 us
  Pallas kernels  150 us (99%)
    pallas_call x1, Pallas kernels, refresh(): pl.pallas_call(kernel, out_shape=(V((GC, SC), F32), V((GC, 128), F32), V(...  147 us
    pallas_call x1, Pallas kernels, finish(): pl.pallas_call(finish_kernel, out_shape=(jax.ShapeDtypeStruct((192, LC),...  3.23 us

profile of v5, /device:TPU:1, one launch (start us, length us, event | category | flops | bytes accessed | tf_op | source)
XLA Modules:
  0.0 151.3 jit_solution(12934006809729234051)
XLA Ops:
  0.6 147.3 %refresh.1 = (f32[1792,896]{1,0:T(8,128)S(1)}, f32[1792,128]{1,0:T(8,128)S(1)}, f32[8,128]{1,0:T(8,128)S(1)}, f32[192,384]{1,0:T(8,128)S(1)}, f32[192,384]{1,0:T(8,128)S(1)}, /*index=5*/f32[8,384]{1,0:T(8,128)S(1)}) custom-call(bf16[4,48,1792]{2,1,0:T(8,128)(2,1)} %bitcast.3, bf16[4,48,384]{2,1,0:T(8,128)(2,1)} %bitcast.5, bf16[2,448,256]{2,1,0:T(8,128)(2,1)} %bitcast.4, ...), custom_call_target="tpu_custom_call" | custom-call | tf_op jit(solution)/shard_map/refresh/pallas_call | solution.py:640
  147.9 3.2 %finish.1 = (f32[192,384]{1,0:T(8,128)}, f32[1792,896]{1,0:T(8,128)}, f32[192,384]{1,0:T(8,128)}, f32[1792,128]{1,0:T(8,128)}) custom-call(f32[1792,896]{1,0:T(8,128)S(1)} %get-tuple-element.10.rnew, f32[1792,128]{1,0:T(8,128)S(1)} %get-tuple-element.11.rprod, f32[8,128]{1,0:T(8,128)S(1)} %get-tuple-element.12.rsum, f32[192,384]{1,0:T(8,128)S(1)} %get-tuple-element.13.lnew, ...), custom_call_target="tpu_custom_call" | custom-call | tf_op jit(solution)/shard_map/finish/pallas_call | solution.py:697

commit v6 on v5

--- a/solution.py
+++ b/solution.py
@@ -536,14 +536,13 @@
             onward(L, 0)
         if u == 15:
             lb(1, 3)
-        if u == 14:
-            late[0].wait()
-            relay_to(3, 11)
-            group_ready(0)
-            gram(0, True, 0, 4)
     relay_to(1, 16)
     lb(3, 6)
     relay_to(2, 16)
+    late[0].wait()
+    relay_to(3, 11)
+    group_ready(0)
+    gram(0, True, 0, 4)
     b_send(2, 2, 0, 1).wait_recv()
     b_send(3, 2, 1, -1).wait_recv()
     begin([], [b_sib(3, 2, k)])
@@ -578,7 +577,6 @@
     make_product(3)
     r0(3)
     r1(2)
-    lb(13, 16)
     r2(0)
     late[1].wait()
     left_refresh()
@@ -590,6 +588,7 @@
     r3(1)
     r2(2)
     total = total + r4(1)
+    lb(13, 16)
     left_product()
     r3(2)
     r2(3)

time: 151 us -> 153 us (1.013)
  Pallas kernels: 150 us -> 152 us
    pallas_call x1, Pallas kernels: 147 us -> 149 us  [refresh(): pl.pallas_call(kernel, out_shape=(V((GC, SC), F32), V((GC, 128), F32), V(...]
where the time goes in v6:
time: 153 us
  Pallas kernels  152 us (99%)
    pallas_call x1, Pallas kernels, refresh(): pl.pallas_call(kernel, out_shape=(V((GC, SC), F32), V((GC, 128), F32), V(...  149 us
    pallas_call x1, Pallas kernels, finish(): pl.pallas_call(finish_kernel, out_shape=(jax.ShapeDtypeStruct((192, LC),...  3.23 us

profile of v6, /device:TPU:1, one launch (start us, length us, event | category | flops | bytes accessed | tf_op | source)
XLA Modules:
  0.0 153.0 jit_solution(14637851183381611389)
XLA Ops:
  0.6 149.0 %refresh.1 = (f32[1792,896]{1,0:T(8,128)S(1)}, f32[1792,128]{1,0:T(8,128)S(1)}, f32[8,128]{1,0:T(8,128)S(1)}, f32[192,384]{1,0:T(8,128)S(1)}, f32[192,384]{1,0:T(8,128)S(1)}, /*index=5*/f32[8,384]{1,0:T(8,128)S(1)}) custom-call(bf16[4,48,1792]{2,1,0:T(8,128)(2,1)} %bitcast.3, bf16[4,48,384]{2,1,0:T(8,128)(2,1)} %bitcast.5, bf16[2,448,256]{2,1,0:T(8,128)(2,1)} %bitcast.4, ...), custom_call_target="tpu_custom_call" | custom-call | tf_op jit(solution)/shard_map/refresh/pallas_call | solution.py:639
  149.6 3.2 %finish.1 = (f32[192,384]{1,0:T(8,128)}, f32[1792,896]{1,0:T(8,128)}, f32[192,384]{1,0:T(8,128)}, f32[1792,128]{1,0:T(8,128)}) custom-call(f32[1792,896]{1,0:T(8,128)S(1)} %get-tuple-element.10.rnew, f32[1792,128]{1,0:T(8,128)S(1)} %get-tuple-element.11.rprod, f32[8,128]{1,0:T(8,128)S(1)} %get-tuple-element.12.rsum, f32[192,384]{1,0:T(8,128)S(1)} %get-tuple-element.13.lnew, ...), custom_call_target="tpu_custom_call" | custom-call | tf_op jit(solution)/shard_map/finish/pallas_call | solution.py:696
